TPU v7x, 512 devices: a whole 4x4x16 slice. The times are simulated.
512 devices in a mesh: expert: 32 (over z, core), row: 16 (over y, x).
Axes of the slice: x: 4, y: 4, z: 16, core: 2. Of those that a mesh axis runs over, the one named last changes fastest.
Arguments:
- grads: bfloat16 [32, 7168, 2048], P('expert', 'row')
- basis: bfloat16 [32, 7168, 256], P('expert', 'row'), may hold values from -0.0625 to 0.0625
- loads: int32 [32], P('expert'), may hold values from 1 to 1, as said below
- flags: int32 [32], P('expert'), may hold values 0 or 1
Outputs:
- new_basis: float32 [32, 7168, 256], P('expert', 'row')
- rotated: float32 [32, 256, 2048], P('expert', None, 'row')
Inputs may be any that keep to these rules, and one draw needn't show every extreme that they name: Slots 0 to loads[d] - 1 of expert-axis index d are live and hold experts; the others are empty. Some index has all 1 slots live.
All inputs are finite; a program needn't handle non-finite values. No bound on the sum of `flags` on one device may be relied on, other than what follows from the above.
Results may differ from a plain program's by a relative error of at most 0.006.
Values sent between devices are 32-bit elements; how exact they have to be, the bound alone decides.
No kernel may reach another device: no remote copies, remote signals or barrier semaphores. Data moves between devices by JAX's collectives and lax.ppermute only.
A program may use at most 64 MiB of HBM per device.

v0:
```python
import jax
import jax.numpy as jnp
from jax import lax
from jax.sharding import Mesh
from jax.sharding import PartitionSpec as P

D = 7168
S = 2048
ROW = ("row_0", "row_1")
EXPERT = ("expert_0", "expert_1")


def copy_for_each(value, axis):
    copies = jnp.broadcast_to(value, (lax.axis_size(axis), *value.shape))
    return lax.all_to_all(copies, axis, split_axis=0, concat_axis=0, tiled=True)


def of_everyone(value, axis):
    return copy_for_each(value, axis).sum(axis=0)


def by_axis(value, axes):
    far, near = axes
    return of_everyone(of_everyone(value, near), far)


def in_one(arrays, axis):
    ends = [0]
    for a in arrays:
        ends.append(ends[-1] + a.size)
    subtotal = by_axis(jnp.concatenate([a.ravel() for a in arrays]), axis)
    return tuple((subtotal[b:e].reshape(a.shape) for a, b, e in zip(arrays, ends, ends[1:])))


def cut_along(value, dim, length):
    dims = value.shape
    parts = value.reshape(*dims[:dim], length, dims[dim] // length, *dims[dim + 1 :])
    return jnp.moveaxis(parts, dim, 0)


def sum_at_owner(value, axis, dim):
    length = lax.axis_size(axis)
    parts = lax.all_to_all(cut_along(value, dim, length), axis, 0, 0, tiled=True)
    return jnp.sum(parts, axis=0)


def rows_for(lines, length):
    spare = -lines.shape[0] % length
    if not spare:
        return lines
    return jnp.concatenate([lines, jnp.zeros((spare, *lines.shape[1:]), lines.dtype)])


def joined_along(parts, dim):
    dims = list(parts.shape[1:])
    dims[dim] *= parts.shape[0]
    return jnp.moveaxis(parts, 0, dim).reshape(dims)


def gather_directly(value, axis, dim):
    return joined_along(copy_for_each(value, axis), dim)


def sum_by_parts(value, axes):
    lines = value.reshape(-1, value.shape[-1])
    own = sum_at_owner(rows_for(lines, lax.axis_size(axes)), axes, 0)
    whole = gather_directly(own, axes, 0)
    return whole[: len(lines)].reshape(value.shape)


def on_device(grads, basis, loads, flags):
    slot_count = grads.shape[0]
    live_count = loads[0]
    live_mask = jnp.arange(slot_count, dtype=jnp.int32) < live_count
    refresh = jnp.logical_and(live_mask, flags == 1)
    live_cube = live_mask[:, None, None]
    refresh_cube = refresh[:, None, None]
    squares = jnp.sum(jnp.where(live_cube, jnp.square(grads.astype(jnp.float32)), 0.0))
    leader = (lax.axis_index(ROW) == 0).astype(jnp.float32)
    total_sq, total_live = in_one(
        (squares, leader * live_count.astype(jnp.float32)),
        (("expert_0", "expert_1"), ("row_0", "row_1")),
    )
    norm_scale = lax.rsqrt(total_sq / (total_live * D * S) + 1e-06)
    local_inner = jnp.einsum("cds,cdk->csk", grads, basis, preferred_element_type=jnp.float32)
    inner_sum = jnp.stack([sum_by_parts(local_inner[0], ROW)])
    inner_gram = jnp.einsum("csk,csj->ckj", inner_sum, inner_sum, precision=lax.Precision.HIGHEST)
    inner_half = inner_sum.astype(jnp.bfloat16)
    power_rows = jnp.einsum(
        "cds,csk->cdk", grads, inner_half, preferred_element_type=jnp.float32
    ).astype(jnp.bfloat16)
    projector = jnp.where(refresh_cube, power_rows, basis)
    local_cross = jnp.einsum("cdk,cds->cks", projector, grads, preferred_element_type=jnp.float32)
    identity = jnp.eye(basis.shape[2], dtype=jnp.float32)
    lower_first = jnp.linalg.cholesky(jnp.where(refresh_cube, inner_gram, identity))
    first_rows = lax.linalg.triangular_solve(
        lower_first, power_rows.astype(jnp.float32), left_side=False, lower=True, transpose_a=True
    )
    local_second = jnp.einsum(
        "cdk,cdj->ckj", first_rows, first_rows, precision=lax.Precision.HIGHEST
    )
    gram_again = sum_by_parts(local_second, ROW)
    cross_cols = sum_at_owner(local_cross, ROW, 2)
    lower_second = jnp.linalg.cholesky(jnp.where(refresh_cube, gram_again, identity))
    fresh_basis = lax.linalg.triangular_solve(
        lower_second, first_rows, left_side=False, lower=True, transpose_a=True
    )
    half_solved = lax.linalg.triangular_solve(lower_first, cross_cols, left_side=True, lower=True)
    fresh_rot = lax.linalg.triangular_solve(lower_second, half_solved, left_side=True, lower=True)
    new_basis = jnp.where(
        refresh_cube, fresh_basis, jnp.where(live_cube, basis.astype(jnp.float32), 0.0)
    )
    rotated = jnp.where(refresh_cube, fresh_rot, jnp.where(live_cube, cross_cols, 0.0)) * norm_scale
    return (new_basis, rotated)


def solution(mesh):
    torus = Mesh(mesh.devices.reshape(16, 2, 4, 4), ("expert_0", "expert_1", "row_0", "row_1"))
    placed = (P(EXPERT, ROW, None), P(EXPERT, ROW, None), P(EXPERT), P(EXPERT))
    return jax.shard_map(
        on_device,
        mesh=torus,
        in_specs=placed,
        out_specs=(P(EXPERT, ROW, None), P(EXPERT, None, ROW)),
        check_vma=False,
    )
```

profile of v0, /device:TPU:6, one launch (start us, length us, event | category | flops | bytes accessed | tf_op | source)
XLA Modules:
  0.0 275.2 jit_solution(10649916008881963235)
XLA Ops:
  0.6 3.6 %fusion.2 = f32[16,128,256]{2,1,0:T(8,128)} fusion(bf16[1,448,256]{2,1,0:T(8,128)(2,1)} %param.10, bf16[1,448,2048]{2,1,0:T(8,128)(2,1)} %param.9), kind=kOutput, calls=%fused_computation.7 | convolution fusion | flops 469762048 | bytes 4161536 | tf_op jit(solution)/shard_map/cds,cdk->csk/dot_general | solution.py:85
  4.2 10.1 %all-to-all-start = ((f32[16,128,256]{2,1,0:T(8,128)}), f32[16,128,256]{2,1,0:T(8,128)}, u32[]{:S(2)}, u32[]{:S(2)}) async-start(f32[16,128,256]{2,1,0:T(8,128)} %fusion.2), calls=%async_computation | async-start | bytes 4194304 | tf_op jit(solution)/shard_map/all_to_all | solution.py:43
  15.0 1.5 select_reduce_fusion
  16.5 0.7 pad_maximum_fusion.2
  17.3 20.5 %all-to-all-done = f32[16,128,256]{2,1,0:T(8,128)} async-done(((f32[16,128,256]{2,1,0:T(8,128)}), f32[16,128,256]{2,1,0:T(8,128)}, u32[]{:S(2)}, u32[]{:S(2)}) %all-to-all-start) | async-done | bytes 2097184 | tf_op jit(solution)/shard_map/all_to_all | solution.py:43
  37.7 0.6 broadcast_in_dim.108
  38.3 7.5 %all-to-all-start.5 = ((f32[16,1,2]{2,1,0:T(1,128)}), f32[16,1,2]{2,1,0:T(1,128)S(1)}, u32[]{:S(2)}, u32[]{:S(2)}) async-start(f32[16,1,2]{2,1,0:T(1,128)} %broadcast_in_dim.108), calls=%async_computation.5 | async-start | bytes 16384 | tf_op jit(solution)/shard_map/all_to_all | solution.py:15
  45.8 1.7 reduce_sum.56
  47.6 3.9 %all-to-all-done.5 = f32[16,1,2]{2,1,0:T(1,128)S(1)} async-done(((f32[16,1,2]{2,1,0:T(1,128)}), f32[16,1,2]{2,1,0:T(1,128)S(1)}, u32[]{:S(2)}, u32[]{:S(2)}) %all-to-all-start.5) | async-done | bytes 160 | tf_op jit(solution)/shard_map/all_to_all | solution.py:15
  51.4 1.6 broadcast_in_dim.98
  53.0 5.6 %all-to-all-start.1 = ((f32[16,128,256]{2,1,0:T(8,128)}), f32[16,128,256]{2,1,0:T(8,128)S(1)}, u32[]{:S(2)}, u32[]{:S(2)}) async-start(f32[16,128,256]{2,1,0:T(8,128)} %broadcast_in_dim.98), calls=%async_computation.1 | async-start | bytes 4194304 | tf_op jit(solution)/shard_map/all_to_all | solution.py:15
  59.3 22.8 %all-to-all-done.1 = f32[16,128,256]{2,1,0:T(8,128)S(1)} async-done(((f32[16,128,256]{2,1,0:T(8,128)}), f32[16,128,256]{2,1,0:T(8,128)S(1)}, u32[]{:S(2)}, u32[]{:S(2)}) %all-to-all-start.1) | async-done | bytes 2097184 | tf_op jit(solution)/shard_map/all_to_all | solution.py:15
  82.1 0.6 broadcast_in_dim.109
  82.7 18.7 %all-to-all-start.6 = ((f32[32,1,2]{2,1,0:T(1,128)}), f32[32,1,2]{2,1,0:T(1,128)S(1)}, u32[]{:S(2)}, u32[]{:S(2)}) async-start(f32[32,1,2]{2,1,0:T(1,128)} %broadcast_in_dim.109), calls=%async_computation.6 | async-start | bytes 32768 | tf_op jit(solution)/shard_map/all_to_all | solution.py:15
  101.4 3.5 %fusion.21 = f32[256,256]{0,1:T(8,128)S(1)} fusion(f32[16,128,256]{2,1,0:T(8,128)S(1)} %all-to-all-done.1, pred[]{:T(512)} %bitcast), kind=kOutput, calls=%fused_computation.25 | convolution fusion | flops 1610809344 | bytes 2359297 | tf_op jit(solution)/shard_map/csk,csj->ckj/dot_general | solution.py:87
  105.1 11.7 %custom-call.21 = f32[1,128,128]{2,1,0:T(8,128)S(1)} custom-call(f32[1,128,128]{2,1,0:T(8,128)S(1)} %cholesky.191), custom_call_target="Cholesky" | custom-call | tf_op jit(solution)/shard_map/jit(cholesky)/cholesky | solution.py:95
  116.8 9.8 %custom-call.22 = f32[1,1,128,128]{2,3,1,0:T(8,128)S(1)} custom-call(f32[1,1,128,128]{3,2,1,0:T(8,128)S(1)} %get-tuple-element.64), custom_call_target="InvertDiagBlocksLowerTriangular" | custom-call | tf_op jit(solution)/shard_map/jit(cholesky)/cholesky | solution.py:95
  127.1 11.9 %custom-call.23 = f32[1,128,128]{2,1,0:T(8,128)S(1)} custom-call(f32[1,128,128]{2,1,0:T(8,128)S(1)} %fusion.22), custom_call_target="Cholesky" | custom-call | tf_op jit(solution)/shard_map/jit(cholesky)/cholesky | solution.py:95
  139.0 0.7 compare_reduce_fusion.2
  141.2 4.1 %while.8 = (s32[]{:T(128)}, f32[1,256,256]{2,1,0:T(8,128)S(1)}, s32[2,2]{1,0:T(2,128)S(1)}, f32[2,1,128,128]{3,2,1,0:T(8,128)S(1)}, s32[]{:T(128)}) while((s32[]{:T(128)}, f32[1,256,256]{2,1,0:T(8,128)S(1)}, s32[2,2]{1,0:T(2,128)S(1)}, f32[2,1,128,128]{3,2,1,0:T(8,128)S(1)}, s32[]{:T(128)}) %tuple.57), condition=%wide.while_cond, body=%wide.while_body.sunk | while | flops 2 | bytes 131181 | solution.py:96
  141.3 0.6 fusion.77
  141.9 1.4 bitcast_dynamic-update-slice_fusion.6
  143.3 0.6 fusion.77
  143.9 1.4 bitcast_dynamic-update-slice_fusion.6
  145.4 0.5 copy-done.9
  145.9 19.7 %custom-call.24 = f32[1,2,128,128]{2,3,1,0:T(8,128)S(1)} custom-call(f32[1,2,128,128]{3,2,1,0:T(8,128)S(1)} %bitcast.256), custom_call_target="InvertDiagBlocksLowerTriangular" | custom-call | tf_op jit(solution)/shard_map/triangular_solve/custom-call.0 | solution.py:96
  165.7 1.4 copy-done.1
  167.1 1.3 fusion.55
  168.4 0.3 fusion.33
  168.8 0.4 fusion.18
  169.1 0.3 convolution_bitcast_fusion.3
  169.8 1.3 fusion.28
  171.1 7.9 %all-to-all-start.2 = ((f32[16,16,256]{2,1,0:T(8,128)}), f32[16,16,256]{2,1,0:T(8,128)S(1)}, u32[]{:S(2)}, u32[]{:S(2)}) async-start(f32[16,16,256]{2,1,0:T(8,128)} %fusion.28), calls=%async_computation.2 | async-start | bytes 524288 | tf_op jit(solution)/shard_map/all_to_all | solution.py:43
  179.0 0.7 fusion.54
  181.0 4.9 %all-to-all-done.2 = f32[16,16,256]{2,1,0:T(8,128)S(1)} async-done(((f32[16,16,256]{2,1,0:T(8,128)}), f32[16,16,256]{2,1,0:T(8,128)S(1)}, u32[]{:S(2)}, u32[]{:S(2)}) %all-to-all-start.2) | async-done | bytes 262176 | tf_op jit(solution)/shard_map/all_to_all | solution.py:43
  185.9 0.7 broadcast_in_dim.99
  186.6 6.0 %all-to-all-start.3 = ((f32[16,16,256]{2,1,0:T(8,128)}), f32[16,16,256]{2,1,0:T(8,128)S(1)}, u32[]{:S(2)}, u32[]{:S(2)}) async-start(f32[16,16,256]{2,1,0:T(8,128)} %broadcast_in_dim.99), calls=%async_computation.3 | async-start | bytes 524288 | tf_op jit(solution)/shard_map/all_to_all | solution.py:15
  192.7 2.1 fusion.6
  194.7 4.2 %all-to-all-done.3 = f32[16,16,256]{2,1,0:T(8,128)S(1)} async-done(((f32[16,16,256]{2,1,0:T(8,128)}), f32[16,16,256]{2,1,0:T(8,128)S(1)}, u32[]{:S(2)}, u32[]{:S(2)}) %all-to-all-start.3) | async-done | bytes 262176 | tf_op jit(solution)/shard_map/all_to_all | solution.py:15
  199.0 6.3 %all-to-all-start.4 = ((f32[16,1,256,128]{3,2,1,0:T(8,128)}), f32[16,1,256,128]{3,2,1,0:T(8,128)S(1)}, u32[]{:S(2)}, u32[]{:S(2)}) async-start(f32[16,1,256,128]{3,2,1,0:T(8,128)} %fusion.6), calls=%async_computation.4 | async-start | bytes 4194304 | tf_op jit(solution)/shard_map/all_to_all | solution.py:43
  205.5 0.8 copy.45
  206.3 1.0 fusion.32
  207.3 0.7 copy-done.6
  208.0 11.7 %custom-call.25 = f32[1,128,128]{2,1,0:T(8,128)S(1)} custom-call(f32[1,128,128]{2,1,0:T(8,128)S(1)} %cholesky.194), custom_call_target="Cholesky" | custom-call | tf_op jit(solution)/shard_map/jit(cholesky)/cholesky | solution.py:104
  219.8 9.8 %custom-call.26 = f32[1,1,128,128]{2,3,1,0:T(8,128)S(1)} custom-call(f32[1,1,128,128]{3,2,1,0:T(8,128)S(1)} %get-tuple-element.60), custom_call_target="InvertDiagBlocksLowerTriangular" | custom-call | tf_op jit(solution)/shard_map/jit(cholesky)/cholesky | solution.py:104
  229.6 1.0 bitcast_dynamic-update-slice_fusion.2
  230.7 1.1 fusion.23
  231.8 11.7 %custom-call.27 = f32[1,128,128]{2,1,0:T(8,128)S(1)} custom-call(f32[1,128,128]{2,1,0:T(8,128)S(1)} %fusion.23), custom_call_target="Cholesky" | custom-call | tf_op jit(solution)/shard_map/jit(cholesky)/cholesky | solution.py:104
  243.5 0.6 compare_reduce_fusion
  244.2 0.6 compare_reduce_fusion.1
  246.1 3.8 %while.9 = (s32[]{:T(128)}, f32[1,256,256]{2,1,0:T(8,128)S(1)}, s32[2,2]{1,0:T(2,128)S(1)}, f32[2,1,128,128]{3,2,1,0:T(8,128)S(1)}, s32[]{:T(128)}) while((s32[]{:T(128)}, f32[1,256,256]{2,1,0:T(8,128)S(1)}, s32[2,2]{1,0:T(2,128)S(1)}, f32[2,1,128,128]{3,2,1,0:T(8,128)S(1)}, s32[]{:T(128)}) %tuple.63), condition=%wide.while_cond.clone, body=%wide.while_body.clone.sunk | while | flops 2 | bytes 131181 | solution.py:105
  246.1 0.6 fusion.78
  246.7 1.3 bitcast_dynamic-update-slice_fusion.7
  248.0 0.6 fusion.78
  248.6 1.3 bitcast_dynamic-update-slice_fusion.7
  249.9 19.9 %custom-call.28 = f32[1,2,128,128]{2,3,1,0:T(8,128)S(1)} custom-call(f32[1,2,128,128]{3,2,1,0:T(8,128)S(1)} %bitcast.257), custom_call_target="InvertDiagBlocksLowerTriangular" | custom-call | tf_op jit(solution)/shard_map/triangular_solve/custom-call.0 | solution.py:105
  269.9 0.3 fusion.34
  270.2 0.4 fusion.20
  270.6 0.3 convolution_bitcast_fusion.1
  270.9 0.8 maximum_select_fusion
  272.2 1.0 fusion.25
  273.7 0.3 fusion.27
  274.0 0.3 convolution_bitcast_fusion.5
  274.3 0.7 fusion.40
  (55 shorter events, 2.6 us)
Async XLA Ops:
  4.2 10.8 %copy-start = (bf16[1,448,2048]{2,1,0:T(8,128)(2,1)S(1)}, bf16[1,448,2048]{2,1,0:T(8,128)(2,1)}, u32[]{:S(2)}) copy-start(bf16[1,448,2048]{2,1,0:T(8,128)(2,1)} %param.9) | copy-start | bytes 5505028
  4.2 33.5 %all-to-all-start = ((f32[16,128,256]{2,1,0:T(8,128)}), f32[16,128,256]{2,1,0:T(8,128)}, u32[]{:S(2)}, u32[]{:S(2)}) async-start(f32[16,128,256]{2,1,0:T(8,128)} %fusion.2), calls=%async_computation | async-start | bytes 4194304 | tf_op jit(solution)/shard_map/all_to_all | solution.py:43
  38.3 13.1 %all-to-all-start.5 = ((f32[16,1,2]{2,1,0:T(1,128)}), f32[16,1,2]{2,1,0:T(1,128)S(1)}, u32[]{:S(2)}, u32[]{:S(2)}) async-start(f32[16,1,2]{2,1,0:T(1,128)} %broadcast_in_dim.108), calls=%async_computation.5 | async-start | bytes 16384 | tf_op jit(solution)/shard_map/all_to_all | solution.py:15
  53.0 29.1 %all-to-all-start.1 = ((f32[16,128,256]{2,1,0:T(8,128)}), f32[16,128,256]{2,1,0:T(8,128)S(1)}, u32[]{:S(2)}, u32[]{:S(2)}) async-start(f32[16,128,256]{2,1,0:T(8,128)} %broadcast_in_dim.98), calls=%async_computation.1 | async-start | bytes 4194304 | tf_op jit(solution)/shard_map/all_to_all | solution.py:15
  82.7 88.4 %all-to-all-start.6 = ((f32[32,1,2]{2,1,0:T(1,128)}), f32[32,1,2]{2,1,0:T(1,128)S(1)}, u32[]{:S(2)}, u32[]{:S(2)}) async-start(f32[32,1,2]{2,1,0:T(1,128)} %broadcast_in_dim.109), calls=%async_computation.6 | async-start | bytes 32768 | tf_op jit(solution)/shard_map/all_to_all | solution.py:15
  145.4 0.5 copy-start.9
  145.4 23.4 %copy-start.4 = (f32[1,256,256]{2,1,0:T(8,128)}, f32[1,256,256]{2,1,0:T(8,128)S(1)}, u32[]{:S(2)}) copy-start(f32[1,256,256]{2,1,0:T(8,128)S(1)} %get-tuple-element.171) | copy-start | bytes 786436
  165.5 3.6 %copy-start.7 = (f32[1,2,128,128]{2,3,1,0:T(8,128)}, f32[1,2,128,128]{2,3,1,0:T(8,128)S(1)}, u32[]{:S(2)}) copy-start(f32[1,2,128,128]{2,3,1,0:T(8,128)S(1)} %custom-call.24) | copy-start | bytes 393220
  165.5 1.5 copy-start.1
  169.5 23.1 %copy-start.2 = (bf16[1,448,2048]{2,1,0:T(8,128)(2,1)S(1)}, bf16[1,448,2048]{2,1,0:T(8,128)(2,1)}, u32[]{:S(2)}) copy-start(bf16[1,448,2048]{2,1,0:T(8,128)(2,1)} %param.9) | copy-start | bytes 5505028
  169.5 23.1 %copy-start.3 = (bf16[1,448,256]{2,1,0:T(8,128)(2,1)S(1)}, bf16[1,448,256]{2,1,0:T(8,128)(2,1)}, u32[]{:S(2)}) copy-start(bf16[1,448,256]{2,1,0:T(8,128)(2,1)} %param.10) | copy-start | bytes 688132
  169.7 22.9 %copy-start.5 = (bf16[1,448,256]{2,1,0:T(8,128)(2,1)S(1)}, bf16[1,448,256]{2,1,0:T(8,128)(2,1)}, u32[]{:S(2)}) copy-start(bf16[1,448,256]{2,1,0:T(8,128)(2,1)} %get-tuple-element.68) | copy-start | bytes 688132
  171.1 14.8 %all-to-all-start.2 = ((f32[16,16,256]{2,1,0:T(8,128)}), f32[16,16,256]{2,1,0:T(8,128)S(1)}, u32[]{:S(2)}, u32[]{:S(2)}) async-start(f32[16,16,256]{2,1,0:T(8,128)} %fusion.28), calls=%async_computation.2 | async-start | bytes 524288 | tf_op jit(solution)/shard_map/all_to_all | solution.py:43
  186.6 12.4 %all-to-all-start.3 = ((f32[16,16,256]{2,1,0:T(8,128)}), f32[16,16,256]{2,1,0:T(8,128)S(1)}, u32[]{:S(2)}, u32[]{:S(2)}) async-start(f32[16,16,256]{2,1,0:T(8,128)} %broadcast_in_dim.99), calls=%async_computation.3 | async-start | bytes 524288 | tf_op jit(solution)/shard_map/all_to_all | solution.py:15
  199.0 72.8 %all-to-all-start.4 = ((f32[16,1,256,128]{3,2,1,0:T(8,128)}), f32[16,1,256,128]{3,2,1,0:T(8,128)S(1)}, u32[]{:S(2)}, u32[]{:S(2)}) async-start(f32[16,1,256,128]{3,2,1,0:T(8,128)} %fusion.6), calls=%async_computation.4 | async-start | bytes 4194304 | tf_op jit(solution)/shard_map/all_to_all | solution.py:43
  205.3 40.8 %copy-start.10 = (s32[2,2]{1,0:T(2,128)S(1)}, s32[2,2]{1,0:T(2,128)}, u32[]{:S(2)}) copy-start(s32[2,2]{1,0:T(2,128)} %copy-done.9) | copy-start | bytes 52
  207.3 0.7 copy-start.6
  270.6 1.3 copy-start.8
where the time goes:
time: 279 us; the launch traced here: 275 us
  other arithmetic  115 us (41%)
  starting transfers between devices  62.1 us (22%)
  waiting for transfers between devices  56.2 us (20%)
  matrix products  18.8 us (7%)
  local copies, waits for them, and re-layouts  16.1 us (6%)
  between operations  6.53 us (2%)
    all_to_all x4, starting transfers between devices, copy_for_each(): return lax.all_to_all(copies, axis, split_axis=0, concat_axis=0, tiled=True)  37.8 us
    another operation x7, other arithmetic, on_device(): jnp.linalg.cholesky(jnp.where(refresh_cube, gram_again, identity))  34.6 us
    another operation x6, other arithmetic, on_device(): jnp.linalg.cholesky(jnp.where(refresh_cube, inner_gram, identity))  34.2 us
    all_to_all x4, waiting for transfers between devices, copy_for_each(): return lax.all_to_all(copies, axis, split_axis=0, concat_axis=0, tiled=True)  30.9 us
    all_to_all x3, waiting for transfers between devices, sum_at_owner(): lax.all_to_all(cut_along(value, dim, length), axis, 0, 0, tiled=True)  25.3 us
    all_to_all x3, starting transfers between devices, sum_at_owner(): lax.all_to_all(cut_along(value, dim, length), axis, 0, 0, tiled=True)  24.3 us
    another operation x2, other arithmetic, on_device(): lax.linalg.triangular_solve(lower_second, first_rows, left_side=False, lo...  20 us
    another operation x3, other arithmetic, on_device(): lax.linalg.triangular_solve(lower_first, power_rows.astype(jnp.float32),...  19.7 us
  transfers between devices with their start and end apart: 7, of which 5 were waited for; matrix products, arithmetic and copies ran while one was open for 50% of the time, Pallas kernels for 0%

commit v1 on v0

v1 whole, which is shorter than its diff:
```python
import functools

import jax
import jax.numpy as jnp
from jax import lax
from jax.experimental import pallas as pl
from jax.experimental.pallas import tpu as pltpu
from jax.sharding import Mesh
from jax.sharding import PartitionSpec as P

ROW = ("row_0", "row_1")
EXPERT = ("expert_0", "expert_1")
F32 = jnp.float32
BF16 = jnp.bfloat16
HIGH = lax.Precision.HIGHEST
BLOCK = 32
NT = (((1,), (1,)), ((), ()))
TN = (((0,), (0,)), ((), ()))
VM = pl.BlockSpec(memory_space=pltpu.VMEM)
SM = pl.BlockSpec(memory_space=pltpu.SMEM)


def cost(flops, nbytes):
    return pl.CostEstimate(flops=int(flops), bytes_accessed=int(nbytes), transcendentals=0)


def product_kernel(extra, left_ref, g_ref, out_ref, lt_ref):
    @pl.when(pl.program_id(0) == 0)
    def _():
        lt_ref[...] = left_ref[...].astype(F32).T.astype(BF16)

    k = lt_ref.shape[0]
    both = jnp.dot(lt_ref[...], g_ref[...], preferred_element_type=F32)
    for h in range(2):
        out_ref[h, :k, :] = both[:, 128 * h : 128 * (h + 1)]
        if extra:
            part = g_ref[:, 128 * h : 128 * (h + 1)].astype(F32)
            out_ref[h, k:, :] = (part * part).reshape(-1, 8, 128).sum(axis=0)


def product(left, g, extra):
    d, k = left.shape
    s = g.shape[1]
    rows = k + extra
    return pl.pallas_call(
        functools.partial(product_kernel, extra),
        grid=(s // 256,),
        in_specs=[pl.BlockSpec((d, k), lambda i: (0, 0)), pl.BlockSpec((d, 256), lambda i: (0, i))],
        out_specs=pl.BlockSpec((2, rows, 128), lambda i: (i, 0, 0)),
        out_shape=jax.ShapeDtypeStruct((s // 128, rows, 128), F32),
        scratch_shapes=[pltpu.VMEM((k, d), BF16)],
        cost_estimate=cost(2 * d * k * s, 2 * d * (s + k) + 4 * rows * s),
        name="product",
    )(left, g)


def spread_kernel(in_ref, out_ref, own_ref):
    total = in_ref[...].sum(axis=0)
    own_ref[...] = total
    out_ref[...] = jnp.broadcast_to(total[None], out_ref.shape)


def spread(parts, steps):
    n, r, c = parts.shape
    b = r // steps
    return pl.pallas_call(
        spread_kernel,
        grid=(steps,),
        in_specs=[pl.BlockSpec((n, b, c), lambda i: (0, i, 0))],
        out_specs=[pl.BlockSpec((n, b, c), lambda i: (0, i, 0)), pl.BlockSpec((b, c), lambda i: (i, 0))],
        out_shape=[jax.ShapeDtypeStruct(parts.shape, F32), jax.ShapeDtypeStruct((r, c), F32)],
        cost_estimate=cost(n * r * c, 8 * n * r * c),
        name="spread",
    )(parts)


def power_of_two(m):
    s = jnp.ones_like(m)
    for e in (64, 32, 16, 8, 4, 2, 1):
        big = m >= 2.0**e
        s = jnp.where(big, s * 2.0**-e, s)
        m = jnp.where(big, m * 2.0**-e, m)
    for e in (64, 32, 16, 8, 4, 2, 1):
        small = m < 2.0 ** (1 - e)
        s = jnp.where(small, s * 2.0 ** (e - 1), s)
        m = jnp.where(small, m * 2.0 ** (e - 1), m)
    return s


def power_kernel(g_ref, w_ref, p_ref, gram_ref, sq_ref):
    n = w_ref.shape[0]
    k = p_ref.shape[1]
    m = jnp.abs(w_ref[0, :k, :])
    sq = w_ref[0, k:, :]
    for j in range(1, n):
        m = jnp.maximum(m, jnp.abs(w_ref[j, :k, :]))
        sq = sq + w_ref[j, k:, :]
    sq_ref[...] = sq
    scale = power_of_two(jnp.max(m, axis=1, keepdims=True))
    acc = jnp.zeros(p_ref.shape, F32)
    for j in range(0, n, 2):
        w = jnp.concatenate([w_ref[j, :k, :], w_ref[j + 1, :k, :]], axis=1)
        w = (w * scale).astype(BF16)
        acc = acc + lax.dot_general(g_ref[:, 128 * j : 128 * j + 256], w, NT, preferred_element_type=F32)
    p = acc.astype(BF16)
    p_ref[...] = p
    pt = p.astype(F32).T.astype(BF16)
    gram_ref[...] = jnp.dot(pt, p, preferred_element_type=F32)


def power(g, w, k):
    d, s = g.shape
    return pl.pallas_call(
        power_kernel,
        in_specs=[VM, VM],
        out_specs=[VM, VM, VM],
        out_shape=[
            jax.ShapeDtypeStruct((d, k), BF16),
            jax.ShapeDtypeStruct((k, k), F32),
            jax.ShapeDtypeStruct((w.shape[1] - k, 128), F32),
        ],
        cost_estimate=cost(2 * d * k * s, 2 * d * s + 4 * k * s),
        name="power",
    )(g, w)


def sub(v, r):
    return jnp.broadcast_to(v[r : r + 1, :], v.shape)


def small_inverse(d):
    groups = BLOCK // 8
    row = lax.broadcasted_iota(jnp.int32, (8, 128), 0)
    lane = lax.broadcasted_iota(jnp.int32, (8, 128), 1)
    x = [jnp.where(lane == row + 8 * g, 1.0, 0.0) for g in range(groups)]
    c = [
        {g: jnp.broadcast_to(d[8 * g : 8 * g + 8, k : k + 1], (8, 128)) for g in range(k // 8, groups)}
        for k in range(BLOCK)
    ]
    for j in range(BLOCK):
        gj, sj = j // 8, j % 8
        r = lax.rsqrt(sub(c[j][gj], sj))
        low = {g: c[j][g] * r for g in range(gj, groups)}
        for k in range(j + 1, BLOCK):
            at = sub(low[k // 8], k % 8)
            for g in range(k // 8, groups):
                c[k][g] = c[k][g] - low[g] * at
        xr = sub(x[gj], sj) * r
        below = jnp.where(row > sj, low[gj], 0.0)
        x[gj] = jnp.where(row == sj, xr, x[gj] - below * xr)
        for g in range(gj + 1, groups):
            x[g] = x[g] - low[g] * xr
    return jnp.concatenate(x, axis=0)


def factor_kernel(refresh_ref, a_ref, p_ref, basis_ref, inv_ref, new_ref, t_ref):
    k = inv_ref.shape[0]
    a = a_ref[...].reshape(k, k)
    lane = lax.broadcasted_iota(jnp.int32, (BLOCK, k), 1)
    row = lax.broadcasted_iota(jnp.int32, (BLOCK, k), 0)
    for b in range(k // BLOCK):
        lo = b * BLOCK
        hi = lo + BLOCK
        r = jnp.where(lane >= lo, a[lo:hi, :], 0.0)
        if b:
            t = t_ref[:lo, :]
            at_lane = lax.broadcasted_iota(jnp.int32, (lo, k), 1)
            at_row = lax.broadcasted_iota(jnp.int32, (lo, k), 0)
            tm = jnp.where(jnp.logical_and(at_lane < lo, at_row < at_lane), 0.0, t)
            r = r - lax.dot_general(t[:, lo:hi], tm, TN, precision=HIGH, preferred_element_type=F32)
        x = small_inverse(r[:, lo:hi])[:, :BLOCK]
        inside = jnp.logical_and(lane >= lo, lane < hi)
        r = jnp.where(inside, jnp.where(lane - lo == row, 1.0, 0.0), r)
        t_ref[lo:hi, :] = jnp.dot(x, r, precision=HIGH, preferred_element_type=F32)
    whole_lane = lax.broadcasted_iota(jnp.int32, (k, k), 1)
    whole_row = lax.broadcasted_iota(jnp.int32, (k, k), 0)
    inv = jnp.where(whole_lane <= whole_row, t_ref[...], 0.0)
    inv_ref[...] = inv
    fresh = lax.dot_general(p_ref[...].astype(F32), inv, NT, precision=HIGH, preferred_element_type=F32)
    old = jnp.where(refresh_ref[1] > 0, basis_ref[...].astype(F32), 0.0)
    new_ref[...] = jnp.where(refresh_ref[0] > 0, fresh, old)


def factor(state, gram, p, basis):
    d, k = p.shape
    return pl.pallas_call(
        factor_kernel,
        in_specs=[SM, VM, VM, VM],
        out_specs=[VM, VM],
        out_shape=[jax.ShapeDtypeStruct((k, k), F32), jax.ShapeDtypeStruct((d, k), F32)],
        scratch_shapes=[pltpu.VMEM((k, k), F32)],
        cost_estimate=cost(6e9, 4 * d * k),
        name="factor",
    )(state, gram, p, basis)


def rotate_kernel(state_ref, scale_ref, parts_ref, inv_ref, stale_ref, out_ref):
    cross = parts_ref[...].sum(axis=0)
    fresh = jnp.dot(inv_ref[...], cross, precision=HIGH, preferred_element_type=F32)
    k = out_ref.shape[0]
    old = jnp.where(state_ref[1] > 0, stale_ref[:k, :], 0.0)
    out_ref[...] = jnp.where(state_ref[0] > 0, fresh, old) * scale_ref[0]


def rotate(state, scale, parts, inv, stale):
    n, k, c = parts.shape
    return pl.pallas_call(
        rotate_kernel,
        in_specs=[SM, SM, VM, VM, VM],
        out_specs=VM,
        out_shape=jax.ShapeDtypeStruct((k, c), F32),
        cost_estimate=cost(2 * k * k * c, 4 * n * k * c),
        name="rotate",
    )(state, scale, parts, inv, stale)


def exchange(blocks, axes):
    return lax.all_to_all(blocks, axes, split_axis=0, concat_axis=0, tiled=True)


def on_device(d_whole, grads, basis, loads, flags):
    g, b = grads[0], basis[0]
    k = b.shape[1]
    s = g.shape[1]
    live = loads[0] >= 1
    refresh = jnp.logical_and(live, flags[0] == 1)
    state = jnp.stack([refresh, live]).astype(jnp.int32)

    parts = product(b, g, 8)
    copies, stale = spread(exchange(parts, ROW), 3)
    p, gram, squares = power(g, exchange(copies, ROW), k)

    n = parts.shape[0]
    gram_copies, _ = spread(exchange(gram.reshape(n, k // n, k), ROW), 1)
    cross = product(p, g, 0)
    whole_gram = exchange(gram_copies, ROW)

    own = jnp.stack([jnp.where(live, squares.sum(), 0.0), live.astype(F32)])
    experts = lax.axis_size(EXPERT)
    totals = exchange(jnp.broadcast_to(own, (experts, 1, 2)), EXPERT).sum(axis=(0, 1))
    norm_scale = lax.rsqrt(totals[0] / (totals[1] * d_whole * s) + 1e-06)

    inv, new_basis = factor(state, whole_gram, p, b)
    rotated = rotate(state, norm_scale.reshape(1), exchange(cross, ROW), inv, stale)
    return new_basis[None], rotated[None]


def solution(mesh):
    torus = Mesh(mesh.devices.reshape(16, 2, 4, 4), EXPERT + ROW)
    placed = (P(EXPERT, ROW, None), P(EXPERT, ROW, None), P(EXPERT), P(EXPERT))

    def whole(grads, basis, loads, flags):
        return jax.shard_map(
            functools.partial(on_device, grads.shape[1]),
            mesh=torus,
            in_specs=placed,
            out_specs=(P(EXPERT, ROW, None), P(EXPERT, None, ROW)),
            check_vma=False,
        )(grads, basis, loads, flags)

    return whole
```

time: 279 us -> 177 us (0.63)
  the two profiles are of different devices: /device:TPU:6 before, /device:TPU:1 now
where the time goes in v1:
time: 177 us; the launch traced here: 176 us
  blocking collectives  62.3 us (35%)
  starting transfers between devices  37.1 us (21%)
  Pallas kernels  36.5 us (21%)
  waiting for transfers between devices  31.4 us (18%)
  between operations  3.9 us (2%)
  local copies, waits for them, and re-layouts  2.59 us (1%)
  other arithmetic  1.99 us (1%)
    all_to_all x2, blocking collectives, exchange(): return lax.all_to_all(blocks, axes, split_axis=0, concat_axis=0, tiled=True)  62.3 us
    all_to_all x4, starting transfers between devices, exchange(): return lax.all_to_all(blocks, axes, split_axis=0, concat_axis=0, tiled=True)  37.1 us
    all_to_all x4, waiting for transfers between devices, exchange(): return lax.all_to_all(blocks, axes, split_axis=0, concat_axis=0, tiled=True)  31.4 us
    pallas_call x2, Pallas kernels, product(): pl.pallas_call(functools.partial(product_kernel, extra), grid=(s // 256,)...  13.3 us
    pallas_call x1, Pallas kernels, factor(): pl.pallas_call(factor_kernel, in_specs=[SM, VM, VM, VM], out_specs=[VM, V...  10.6 us
    pallas_call x2, Pallas kernels, spread(): pl.pallas_call(spread_kernel, grid=(steps,), in_specs=[pl.BlockSpec((n, b...  5.57 us
    pallas_call x1, Pallas kernels, power(): pl.pallas_call(power_kernel, in_specs=[VM, VM], out_specs=[VM, VM, VM], o...  4.22 us
  transfers between devices with their start and end apart: 4, of which 4 were waited for; matrix products, arithmetic and copies ran while one was open for 1% of the time, Pallas kernels for 11%

profile of v1, /device:TPU:1, one launch (start us, length us, event | category | flops | bytes accessed | tf_op | source)
XLA Modules:
  0.0 175.8 jit_solution(457736960332559968)
XLA Ops:
  0.6 6.7 %product.2 = f32[16,264,128]{2,1,0:T(8,128)} custom-call(bf16[448,256]{1,0:T(8,128)(2,1)} %bitcast.13, bf16[448,2048]{1,0:T(8,128)(2,1)} %bitcast.9), custom_call_target="tpu_custom_call" | custom-call | flops 469762048 | bytes 4227072 | tf_op jit(solution)/shard_map/product/pallas_call | solution.py:45
  7.3 33.1 %all_to_all.30.in_ref = f32[16,264,128]{2,1,0:T(8,128)} all-to-all(f32[16,264,128]{2,1,0:T(8,128)} %product.2), channel_id=1, replica_groups=mesh['expert_0'=16,'expert_1'=2,'row_0'=4,'row_1'=4] {'row_0','row_1'}, dimensions={0} | all-to-all | bytes 4325376 | tf_op jit(solution)/shard_map/all_to_all | solution.py:218
  40.4 3.9 %spread.2 = (f32[16,264,128]{2,1,0:T(8,128)}, f32[264,128]{1,0:T(8,128)}) custom-call(f32[16,264,128]{2,1,0:T(8,128)} %all_to_all.30.in_ref), custom_call_target="tpu_custom_call" | custom-call | flops 540672 | bytes 4325376 | tf_op jit(solution)/shard_map/spread/pallas_call | solution.py:66
  44.3 29.2 %all_to_all.31.w_ref = f32[16,264,128]{2,1,0:T(8,128)} all-to-all(f32[16,264,128]{2,1,0:T(8,128)} %get-tuple-element.10), channel_id=1, replica_groups=mesh['expert_0'=16,'expert_1'=2,'row_0'=4,'row_1'=4] {'row_0','row_1'}, dimensions={0} | all-to-all | bytes 4325376 | tf_op jit(solution)/shard_map/all_to_all | solution.py:218
  73.5 4.2 %power.1 = (bf16[448,256]{1,0:T(8,128)(2,1)}, f32[256,256]{1,0:T(8,128)}, f32[8,128]{1,0:T(8,128)}) custom-call(bf16[448,2048]{1,0:T(8,128)(2,1)} %bitcast.10, f32[16,264,128]{2,1,0:T(8,128)} %all_to_all.31.w_ref), custom_call_target="tpu_custom_call" | custom-call | flops 469762048 | bytes 3932160 | tf_op jit(solution)/shard_map/power/pallas_call | solution.py:113
  77.7 3.5 %all-to-all-start.2 = ((f32[16,16,256]{2,1,0:T(8,128)}), f32[16,16,256]{2,1,0:T(8,128)S(1)}, u32[]{:S(2)}, u32[]{:S(2)}) async-start(f32[16,16,256]{2,1,0:T(8,128)} %bitcast.12), calls=%async_computation.2 | async-start | bytes 524288 | tf_op jit(solution)/shard_map/all_to_all | solution.py:218
  81.9 1.3 reduce_sum.18
  83.7 0.1 pad_maximum_fusion
  83.8 4.9 %all-to-all-done.2.in_ref = f32[16,16,256]{2,1,0:T(8,128)S(1)} async-done(((f32[16,16,256]{2,1,0:T(8,128)}), f32[16,16,256]{2,1,0:T(8,128)S(1)}, u32[]{:S(2)}, u32[]{:S(2)}) %all-to-all-start.2) | async-done | bytes 262176 | tf_op jit(solution)/shard_map/all_to_all | solution.py:218
  88.7 0.0 copy-start.1
  88.7 0.7 broadcast_in_dim.10
  89.4 24.6 %all-to-all-start.4 = ((f32[32,1,2]{2,1,0:T(1,128)}), f32[32,1,2]{2,1,0:T(1,128)S(1)}, u32[]{:S(2)}, u32[]{:S(2)}) async-start(f32[32,1,2]{2,1,0:T(1,128)} %broadcast_in_dim.10), calls=%async_computation.4 | async-start | bytes 32768 | tf_op jit(solution)/shard_map/all_to_all | solution.py:218
  114.0 0.0 copy-done.1
  114.0 1.7 spread.3
  115.7 10.1 %all-to-all-done.4 = f32[32,1,2]{2,1,0:T(1,128)S(1)} async-done(((f32[32,1,2]{2,1,0:T(1,128)}), f32[32,1,2]{2,1,0:T(1,128)S(1)}, u32[]{:S(2)}, u32[]{:S(2)}) %all-to-all-start.4) | async-done | bytes 288 | tf_op jit(solution)/shard_map/all_to_all | solution.py:218
  125.8 3.5 %all-to-all-start.3 = ((f32[16,16,256]{2,1,0:T(8,128)}), f32[16,16,256]{2,1,0:T(8,128)S(1)}, u32[]{:S(2)}, u32[]{:S(2)}) async-start(f32[16,16,256]{2,1,0:T(8,128)} %get-tuple-element.12), calls=%async_computation.3 | async-start | bytes 524288 | tf_op jit(solution)/shard_map/all_to_all | solution.py:218
  129.3 6.7 %product.3 = f32[16,256,128]{2,1,0:T(8,128)} custom-call(bf16[448,256]{1,0:T(8,128)(2,1)} %get-tuple-element.13.p_ref.left_ref, bf16[448,2048]{1,0:T(8,128)(2,1)} %bitcast.11), custom_call_target="tpu_custom_call" | custom-call | flops 469762048 | bytes 4161536 | tf_op jit(solution)/shard_map/product/pallas_call | solution.py:45
  136.0 1.1 all-to-all-done.3.a_ref
  137.1 0.0 copy-start.2
  137.1 5.5 %all-to-all-start.5 = ((f32[16,256,128]{2,1,0:T(8,128)}), f32[16,256,128]{2,1,0:T(8,128)S(1)}, u32[]{:S(2)}, u32[]{:S(2)}) async-start(f32[16,256,128]{2,1,0:T(8,128)} %product.3), calls=%async_computation.5 | async-start | bytes 4194304 | tf_op jit(solution)/shard_map/all_to_all | solution.py:218
  143.2 0.6 add_convert_fusion.refresh_ref.state_ref
  143.8 0.1 reduce_sum.19
  143.9 0.6 fusion
  145.8 0.0 copy-done.2
  145.8 10.6 %factor.1 = (f32[256,256]{1,0:T(8,128)}, f32[448,256]{1,0:T(8,128)}) custom-call(s32[2]{0:T(128)} %add_convert_fusion.refresh_ref.state_ref, f32[16,16,256]{2,1,0:T(8,128)} %copy-done.2, bf16[448,256]{1,0:T(8,128)(2,1)} %get-tuple-element.13.p_ref.left_ref, bf16[448,256]{1,0:T(8,128)(2,1)} %bitcast.14), custom_call_target="tpu_custom_call" | custom-call | flops 6000000000 | bytes 458752 | tf_op jit(solution)/shard_map/factor/pallas_call | solution.py:186
  156.4 15.3 %all-to-all-done.5.parts_ref = f32[16,256,128]{2,1,0:T(8,128)S(1)} async-done(((f32[16,256,128]{2,1,0:T(8,128)}), f32[16,256,128]{2,1,0:T(8,128)S(1)}, u32[]{:S(2)}, u32[]{:S(2)}) %all-to-all-start.5) | async-done | bytes 2097184 | tf_op jit(solution)/shard_map/all_to_all | solution.py:218
  171.7 0.0 copy-start
  171.7 1.3 copy-done
  173.0 2.8 %rotate.1 = f32[256,128]{1,0:T(8,128)} custom-call(s32[2]{0:T(128)} %add_convert_fusion.refresh_ref.state_ref, f32[1]{0:T(128)S(6)} %rsqrt.4.scale_ref, f32[16,256,128]{2,1,0:T(8,128)} %copy-done, f32[256,256]{1,0:T(8,128)} %get-tuple-element.16.inv_ref, f32[264,128]{1,0:T(8,128)} %get-tuple-element.17.stale_ref), custom_call_target="tpu_custom_call" | custom-call | flops 16777216 | bytes 2097152 | tf_op jit(solution)/shard_map/rotate/pallas_call | solution.py:207
Async XLA Ops:
  77.7 11.0 %all-to-all-start.2 = ((f32[16,16,256]{2,1,0:T(8,128)}), f32[16,16,256]{2,1,0:T(8,128)S(1)}, u32[]{:S(2)}, u32[]{:S(2)}) async-start(f32[16,16,256]{2,1,0:T(8,128)} %bitcast.12), calls=%async_computation.2 | async-start | bytes 524288 | tf_op jit(solution)/shard_map/all_to_all | solution.py:218
  88.7 25.3 %copy-start.1 = (f32[16,16,256]{2,1,0:T(8,128)}, f32[16,16,256]{2,1,0:T(8,128)S(1)}, u32[]{:S(2)}) copy-start(f32[16,16,256]{2,1,0:T(8,128)S(1)} %all-to-all-done.2.in_ref) | copy-start | bytes 786436
  89.4 36.4 %all-to-all-start.4 = ((f32[32,1,2]{2,1,0:T(1,128)}), f32[32,1,2]{2,1,0:T(1,128)S(1)}, u32[]{:S(2)}, u32[]{:S(2)}) async-start(f32[32,1,2]{2,1,0:T(1,128)} %broadcast_in_dim.10), calls=%async_computation.4 | async-start | bytes 32768 | tf_op jit(solution)/shard_map/all_to_all | solution.py:218
  125.8 11.3 %all-to-all-start.3 = ((f32[16,16,256]{2,1,0:T(8,128)}), f32[16,16,256]{2,1,0:T(8,128)S(1)}, u32[]{:S(2)}, u32[]{:S(2)}) async-start(f32[16,16,256]{2,1,0:T(8,128)} %get-tuple-element.12), calls=%async_computation.3 | async-start | bytes 524288 | tf_op jit(solution)/shard_map/all_to_all | solution.py:218
  137.1 8.7 %copy-start.2 = (f32[16,16,256]{2,1,0:T(8,128)}, f32[16,16,256]{2,1,0:T(8,128)S(1)}, u32[]{:S(2)}) copy-start(f32[16,16,256]{2,1,0:T(8,128)S(1)} %all-to-all-done.3.a_ref) | copy-start | bytes 786436
  137.1 34.6 %all-to-all-start.5 = ((f32[16,256,128]{2,1,0:T(8,128)}), f32[16,256,128]{2,1,0:T(8,128)S(1)}, u32[]{:S(2)}, u32[]{:S(2)}) async-start(f32[16,256,128]{2,1,0:T(8,128)} %product.3), calls=%async_computation.5 | async-start | bytes 4194304 | tf_op jit(solution)/shard_map/all_to_all | solution.py:218
  171.7 1.3 copy-start

commit v2 on v1

v2 whole, which is shorter than its diff:
```python
import functools

import jax
import jax.numpy as jnp
from jax import lax
from jax.experimental import pallas as pl
from jax.experimental.pallas import tpu as pltpu
from jax.sharding import Mesh
from jax.sharding import PartitionSpec as P

ROW = ("row_0", "row_1")
EXPERT = ("expert_0", "expert_1")
F32 = jnp.float32
BF16 = jnp.bfloat16
HIGH = lax.Precision.HIGHEST
BLOCK = 32
STAGGER = 9000
NT = (((1,), (1,)), ((), ()))
TN = (((0,), (0,)), ((), ()))
VM = pl.BlockSpec(memory_space=pltpu.VMEM)
SM = pl.BlockSpec(memory_space=pltpu.SMEM)
HBM = pl.BlockSpec(memory_space=pltpu.HBM)


def cost(flops, nbytes):
    return pl.CostEstimate(flops=int(flops), bytes_accessed=int(nbytes), transcendentals=0)


def params():
    return pltpu.CompilerParams(vmem_limit_bytes=16 * 1024 * 1024)


def product_columns(lt, g_ref, i):
    return jnp.dot(lt, g_ref[:, 256 * i : 256 * (i + 1)], preferred_element_type=F32)


def put(both, held_ref, out_ref, sem, i):
    k = both.shape[0]
    for h in range(2):
        held_ref[2 * i + h] = both[:, 128 * h : 128 * (h + 1)]
    copy = pltpu.make_async_copy(
        held_ref.at[pl.ds(2 * i, 2)], out_ref.at[pl.ds(2 * i, 2), pl.ds(0, k), :], sem.at[i]
    )
    copy.start()
    return copy


def first_kernel(state_ref, left_hbm, g_hbm, out_ref, left_ref, g_ref, held_ref, extra_ref, in_sem, out_sem):
    n, k, _ = held_ref.shape
    pairs = n // 2
    left_copy = pltpu.make_async_copy(left_hbm, left_ref, in_sem.at[pairs])
    left_copy.start()
    loads = []
    for i in range(pairs):
        cols = pl.ds(256 * i, 256)
        loads.append(pltpu.make_async_copy(g_hbm.at[:, cols], g_ref.at[:, cols], in_sem.at[i]))
        loads[-1].start()

    @pl.when(state_ref[2] > 0)
    def _():
        pl.delay(STAGGER)

    left_copy.wait()
    lt = left_ref[...].astype(F32).T.astype(BF16)
    squares = jnp.zeros((8, 256), F32)
    stores = []
    for i in range(pairs):
        loads[i].wait()
        stores.append(put(product_columns(lt, g_ref, i), held_ref, out_ref, out_sem, i))
        part = g_ref[:, 256 * i : 256 * (i + 1)].astype(F32)
        squares = squares + (part * part).reshape(-1, 8, 256).sum(axis=0)
    live = state_ref[1] > 0
    squares = jnp.where(live, squares[:, :128] + squares[:, 128:], 0.0)
    slot = jnp.where(live, jnp.full((8, 128), 1.0 / (8 * 128 * n), F32), 0.0)
    for j in range(n):
        extra_ref[j, :8, :] = squares
        extra_ref[j, 8:, :] = slot
    last = pltpu.make_async_copy(extra_ref, out_ref.at[:, pl.ds(k, 16), :], out_sem.at[pairs])
    last.start()
    for copy in stores:
        copy.wait()
    last.wait()


def first(state, left, g):
    d, k = left.shape
    s = g.shape[1]
    n = s // 128
    return pl.pallas_call(
        first_kernel,
        in_specs=[SM, HBM, HBM],
        out_specs=HBM,
        out_shape=pltpu.HBM((n, k + 16, 128), F32),
        scratch_shapes=[
            pltpu.VMEM((d, k), BF16),
            pltpu.VMEM((d, s), BF16),
            pltpu.VMEM((n, k, 128), F32),
            pltpu.VMEM((n, 16, 128), F32),
            pltpu.SemaphoreType.DMA((n // 2 + 1,)),
            pltpu.SemaphoreType.DMA((n // 2 + 1,)),
        ],
        compiler_params=params(),
        cost_estimate=cost(2 * d * k * s, 2 * d * (s + k) + 4 * k * s),
        name="first",
    )(state, pltpu.with_memory_space_constraint(left, pltpu.HBM), pltpu.with_memory_space_constraint(g, pltpu.HBM))


def second_kernel(left_ref, g_ref, out_ref, held_ref, sem):
    lt = left_ref[...].astype(F32).T.astype(BF16)
    n = held_ref.shape[0]
    stores = [put(product_columns(lt, g_ref, i), held_ref, out_ref, sem, i) for i in range(n // 2)]
    for copy in stores:
        copy.wait()


def second(left, g):
    d, k = left.shape
    s = g.shape[1]
    n = s // 128
    return pl.pallas_call(
        second_kernel,
        in_specs=[VM, VM],
        out_specs=HBM,
        out_shape=pltpu.HBM((n, k, 128), F32),
        scratch_shapes=[pltpu.VMEM((n, k, 128), F32), pltpu.SemaphoreType.DMA((n // 2,))],
        compiler_params=params(),
        cost_estimate=cost(2 * d * k * s, 2 * d * (s + k) + 4 * k * s),
        name="second",
    )(left, g)


def spread_kernel(kept, in_ref, own_ref, out_ref, sem):
    n = in_ref.shape[0]
    rows = out_ref.shape[1]
    step = rows // (1 if rows < 64 else 4)
    copies = []
    for c in range(rows // step):
        at = pl.ds(c * step, step)
        own_ref[at, :] = in_ref[:, at, :].sum(axis=0)
        for j in range(n):
            copies.append(pltpu.make_async_copy(own_ref.at[at], out_ref.at[j, at], sem.at[c, j]))
            copies[-1].start()
    if kept:
        own_ref[rows:, :] = in_ref[:, rows:, :].sum(axis=0)
    for copy in copies:
        copy.wait()


def spread(parts, kept):
    n, r, c = parts.shape
    return pl.pallas_call(
        functools.partial(spread_kernel, kept),
        in_specs=[VM],
        out_specs=[VM, HBM],
        out_shape=[jax.ShapeDtypeStruct((r, c), F32), pltpu.HBM((n, r - kept, c), F32)],
        scratch_shapes=[pltpu.SemaphoreType.DMA((4, n))],
        compiler_params=params(),
        cost_estimate=cost(n * r * c, 8 * n * r * c),
        name="spread",
    )(parts)


def power_of_two(m):
    s = jnp.ones_like(m)
    for e in (64, 32, 16, 8, 4, 2, 1):
        big = m >= 2.0**e
        s = jnp.where(big, s * 2.0**-e, s)
        m = jnp.where(big, m * 2.0**-e, m)
    for e in (64, 32, 16, 8, 4, 2, 1):
        small = m < 2.0 ** (1 - e)
        s = jnp.where(small, s * 2.0 ** (e - 1), s)
        m = jnp.where(small, m * 2.0 ** (e - 1), m)
    return s


def power_kernel(g_ref, w_ref, extra_ref, p_ref, gram_ref):
    n = w_ref.shape[0]
    k = p_ref.shape[1]
    m = jnp.abs(w_ref[0])
    for j in range(1, n):
        m = jnp.maximum(m, jnp.abs(w_ref[j]))
    scale = power_of_two(jnp.max(m, axis=1, keepdims=True))
    acc = jnp.zeros(p_ref.shape, F32)
    for j in range(0, n, 2):
        w = jnp.concatenate([w_ref[j], w_ref[j + 1]], axis=1)
        w = (w * scale).astype(BF16)
        acc = acc + lax.dot_general(g_ref[:, 128 * j : 128 * j + 256], w, NT, preferred_element_type=F32)
    p = acc.astype(BF16)
    p_ref[...] = p
    pt = p.astype(F32).T.astype(BF16)
    gram = jnp.dot(pt, p, preferred_element_type=F32)
    gram_ref[:, : k // n, :] = gram.reshape(n, k // n, k)
    extra = jnp.concatenate([extra_ref[:8, :], extra_ref[8:, :]], axis=1)
    for j in range(n):
        gram_ref[j, k // n :, :] = extra


def power(g, w, extra):
    d, s = g.shape
    n, k, _ = w.shape
    return pl.pallas_call(
        power_kernel,
        in_specs=[VM, VM, VM],
        out_specs=[VM, VM],
        out_shape=[jax.ShapeDtypeStruct((d, k), BF16), jax.ShapeDtypeStruct((n, k // n + 8, k), F32)],
        compiler_params=params(),
        cost_estimate=cost(2 * d * k * s, 2 * d * s + 4 * k * s),
        name="power",
    )(g, w, extra)


def sub(v, r):
    return jnp.broadcast_to(v[r : r + 1, :], v.shape)


def small_inverse(d):
    groups = BLOCK // 8
    row = lax.broadcasted_iota(jnp.int32, (8, 128), 0)
    lane = lax.broadcasted_iota(jnp.int32, (8, 128), 1)
    x = [jnp.where(lane == row + 8 * g, 1.0, 0.0) for g in range(groups)]
    c = [
        {g: jnp.broadcast_to(d[8 * g : 8 * g + 8, k : k + 1], (8, 128)) for g in range(k // 8, groups)}
        for k in range(BLOCK)
    ]
    for j in range(BLOCK):
        gj, sj = j // 8, j % 8
        r = lax.rsqrt(sub(c[j][gj], sj))
        low = {g: c[j][g] * r for g in range(gj, groups)}
        for k in range(j + 1, BLOCK):
            at = sub(low[k // 8], k % 8)
            for g in range(k // 8, groups):
                c[k][g] = c[k][g] - low[g] * at
        xr = sub(x[gj], sj) * r
        below = jnp.where(row > sj, low[gj], 0.0)
        x[gj] = jnp.where(row == sj, xr, x[gj] - below * xr)
        for g in range(gj + 1, groups):
            x[g] = x[g] - low[g] * xr
    return jnp.concatenate(x, axis=0)


def factor_kernel(refresh_ref, a_ref, p_ref, basis_ref, inv_ref, new_ref, t_ref):
    k = inv_ref.shape[0]
    a = a_ref[...].reshape(k, k)
    lane = lax.broadcasted_iota(jnp.int32, (BLOCK, k), 1)
    row = lax.broadcasted_iota(jnp.int32, (BLOCK, k), 0)
    for b in range(k // BLOCK):
        lo = b * BLOCK
        hi = lo + BLOCK
        r = jnp.where(lane >= lo, a[lo:hi, :], 0.0)
        if b:
            t = t_ref[:lo, :]
            at_lane = lax.broadcasted_iota(jnp.int32, (lo, k), 1)
            at_row = lax.broadcasted_iota(jnp.int32, (lo, k), 0)
            tm = jnp.where(jnp.logical_and(at_lane < lo, at_row < at_lane), 0.0, t)
            r = r - lax.dot_general(t[:, lo:hi], tm, TN, precision=HIGH, preferred_element_type=F32)
        x = small_inverse(r[:, lo:hi])[:, :BLOCK]
        inside = jnp.logical_and(lane >= lo, lane < hi)
        r = jnp.where(inside, jnp.where(lane - lo == row, 1.0, 0.0), r)
        t_ref[lo:hi, :] = jnp.dot(x, r, precision=HIGH, preferred_element_type=F32)
    whole_lane = lax.broadcasted_iota(jnp.int32, (k, k), 1)
    whole_row = lax.broadcasted_iota(jnp.int32, (k, k), 0)
    inv = jnp.where(whole_lane <= whole_row, t_ref[...], 0.0)
    inv_ref[...] = inv
    fresh = lax.dot_general(p_ref[...].astype(F32), inv, NT, precision=HIGH, preferred_element_type=F32)
    old = jnp.where(refresh_ref[1] > 0, basis_ref[...].astype(F32), 0.0)
    new_ref[...] = jnp.where(refresh_ref[0] > 0, fresh, old)


def factor(state, gram, p, basis):
    d, k = p.shape
    return pl.pallas_call(
        factor_kernel,
        in_specs=[SM, VM, VM, VM],
        out_specs=[VM, VM],
        out_shape=[jax.ShapeDtypeStruct((k, k), F32), jax.ShapeDtypeStruct((d, k), F32)],
        scratch_shapes=[pltpu.VMEM((k, k), F32)],
        compiler_params=params(),
        cost_estimate=cost(6e9, 4 * d * k),
        name="factor",
    )(state, gram, p, basis)


def rotate_kernel(size, state_ref, sums_ref, parts_ref, inv_ref, stale_ref, out_ref):
    fresh = jnp.dot(inv_ref[...], parts_ref[...].sum(axis=0), precision=HIGH, preferred_element_type=F32)
    squares = jnp.sum(sums_ref[:, :128], axis=(0, 1), keepdims=True)
    slots = jnp.sum(sums_ref[:, 128:], axis=(0, 1), keepdims=True)
    scale = lax.rsqrt(squares / (slots * size) + 1e-06)
    old = jnp.where(state_ref[1] > 0, stale_ref[...], 0.0)
    out_ref[...] = jnp.where(state_ref[0] > 0, fresh, old) * scale


def rotate(size, state, sums, parts, inv, stale):
    n, k, c = parts.shape
    return pl.pallas_call(
        functools.partial(rotate_kernel, size),
        in_specs=[SM, VM, VM, VM, VM],
        out_specs=VM,
        out_shape=jax.ShapeDtypeStruct((k, c), F32),
        compiler_params=params(),
        cost_estimate=cost(2 * k * k * c, 4 * n * k * c),
        name="rotate",
    )(state, sums, parts, inv, stale)


def exchange(blocks, axes):
    return lax.all_to_all(blocks, axes, split_axis=0, concat_axis=0, tiled=True)


def between_planes(value):
    far = lax.axis_size(EXPERT[0])
    rows = lax.axis_size(ROW)
    pairs = [(z * rows + r, (z + r) % far * rows + r) for z in range(far) for r in range(rows)]
    return lax.ppermute(value, (EXPERT[0],) + ROW, pairs)


def both_cores(value):
    return value + lax.ppermute(value, EXPERT[1], [(0, 1), (1, 0)])


def on_device(d_whole, grads, basis, loads, flags):
    g, b = grads[0], basis[0]
    k = b.shape[1]
    s = g.shape[1]
    live = loads[0] >= 1
    refresh = jnp.logical_and(live, flags[0] == 1)
    late = lax.axis_index(EXPERT[1]) == 0
    state = jnp.stack([refresh, live, late]).astype(jnp.int32)

    received = exchange(first(state, b, g), ROW)
    n = received.shape[0]
    own, copies = spread(received, 16)
    stale, plane = own[:k], own[k:]
    planes = between_planes(plane)
    received, planes = lax.optimization_barrier((exchange(copies, ROW), planes))
    p, gram = power(g, received, planes)
    own, gram_copies = spread(exchange(gram, ROW), 8)
    cross = second(p, g)
    whole_gram = exchange(gram_copies, ROW)
    inv, new_basis = factor(state, whole_gram, p, b)
    inv, core = lax.optimization_barrier((inv, own[k // n :]))
    rotated = rotate(float(d_whole * s), state, both_cores(core), exchange(cross, ROW), inv, stale)
    return new_basis[None], rotated[None]


def solution(mesh):
    torus = Mesh(mesh.devices.reshape(16, 2, 4, 4), EXPERT + ROW)
    placed = (P(EXPERT, ROW, None), P(EXPERT, ROW, None), P(EXPERT), P(EXPERT))

    def whole(grads, basis, loads, flags):
        return jax.shard_map(
            functools.partial(on_device, grads.shape[1]),
            mesh=torus,
            in_specs=placed,
            out_specs=(P(EXPERT, ROW, None), P(EXPERT, None, ROW)),
            check_vma=False,
        )(grads, basis, loads, flags)

    return whole
```

time: 177 us -> 130 us (0.73)
  the two profiles are of different devices: /device:TPU:1 before, /device:TPU:480 now
where the time goes in v2:
time: 130 us
  blocking collectives  41.5 us (32%)
  waiting for transfers between devices  39 us (30%)
  Pallas kernels  32.4 us (25%)
  starting transfers between devices  14.4 us (11%)
  between operations  2.07 us (2%)
    all_to_all x2, blocking collectives, exchange(): return lax.all_to_all(blocks, axes, split_axis=0, concat_axis=0, tiled=True)  41.5 us
    all_to_all x3, waiting for transfers between devices, exchange(): return lax.all_to_all(blocks, axes, split_axis=0, concat_axis=0, tiled=True)  37.9 us
    pallas_call x1, Pallas kernels, first(): pl.pallas_call(first_kernel, in_specs=[SM, HBM, HBM], out_specs=HBM, out_...  12.9 us
    all_to_all x3, starting transfers between devices, exchange(): return lax.all_to_all(blocks, axes, split_axis=0, concat_axis=0, tiled=True)  11.8 us
    pallas_call x1, Pallas kernels, factor(): pl.pallas_call(factor_kernel, in_specs=[SM, VM, VM, VM], out_specs=[VM, V...  9.97 us
    pallas_call x2, Pallas kernels, spread(): pl.pallas_call(functools.partial(spread_kernel, kept), in_specs=[VM], out...  3.22 us
    pallas_call x1, Pallas kernels, power(): pl.pallas_call(power_kernel, in_specs=[VM, VM, VM], out_specs=[VM, VM], o...  2.93 us
  transfers between devices with their start and end apart: 5, of which 4 were waited for; matrix products, arithmetic and copies ran while one was open for 0% of the time, Pallas kernels for 9%

profile of v2, /device:TPU:480, one launch (start us, length us, event | category | flops | bytes accessed | tf_op | source)
XLA Modules:
  0.0 129.5 jit_solution(12154251582004876420)
XLA Ops:
  1.9 0.1 add_convert_fusion.state_ref.refresh_ref
  2.0 12.9 %first.1 = f32[16,272,128]{2,1,0:T(8,128)} custom-call(s32[3]{0:T(128)S(1)} %add_convert_fusion.state_ref.refresh_ref, bf16[448,256]{1,0:T(8,128)(2,1)} %bitcast.8, bf16[448,2048]{1,0:T(8,128)(2,1)} %bitcast.5), custom_call_target="tpu_custom_call" | custom-call | flops 469762048 | bytes 4161536 | tf_op jit(solution)/shard_map/first/pallas_call | solution.py:89
  14.9 29.0 %all_to_all.25.in_ref = f32[16,272,128]{2,1,0:T(8,128)S(1)} all-to-all(f32[16,272,128]{2,1,0:T(8,128)} %first.1), channel_id=1, replica_groups=mesh['expert_0'=16,'expert_1'=2,'row_0'=4,'row_1'=4] {'row_0','row_1'}, dimensions={0} | all-to-all | bytes 4456448 | tf_op jit(solution)/shard_map/all_to_all | solution.py:306
  43.9 1.9 %spread.2 = (f32[272,128]{1,0:T(8,128)S(1)}, f32[16,256,128]{2,1,0:T(8,128)}) custom-call(f32[16,272,128]{2,1,0:T(8,128)S(1)} %all_to_all.25.in_ref), custom_call_target="tpu_custom_call" | custom-call | flops 557056 | bytes 4456448 | tf_op jit(solution)/shard_map/spread/pallas_call | solution.py:151
  45.8 0.0 copy-start
  45.8 4.6 %all-to-all-start.1 = ((f32[16,256,128]{2,1,0:T(8,128)}), f32[16,256,128]{2,1,0:T(8,128)}, u32[]{:S(2)}, u32[]{:S(2)}) async-start(f32[16,256,128]{2,1,0:T(8,128)} %get-tuple-element.14), calls=%async_computation.1 | async-start | bytes 4194304 | tf_op jit(solution)/shard_map/all_to_all | solution.py:306
  50.4 0.7 collective-permute-start
  51.1 0.0 collective-permute-done.extra_ref
  51.1 21.7 %all-to-all-done.1.w_ref = f32[16,256,128]{2,1,0:T(8,128)} async-done(((f32[16,256,128]{2,1,0:T(8,128)}), f32[16,256,128]{2,1,0:T(8,128)}, u32[]{:S(2)}, u32[]{:S(2)}) %all-to-all-start.1) | async-done | bytes 2097184 | tf_op jit(solution)/shard_map/all_to_all | solution.py:306
  72.8 0.0 copy-done
  72.8 2.9 %power.1 = (bf16[448,256]{1,0:T(8,128)(2,1)S(1)}, f32[16,24,256]{2,1,0:T(8,128)S(1)}) custom-call(bf16[448,2048]{1,0:T(8,128)(2,1)S(1)} %bitcast.6, f32[16,256,128]{2,1,0:T(8,128)} %all-to-all-done.1.w_ref, f32[16,128]{1,0:T(8,128)S(1)} %collective-permute-done.extra_ref), custom_call_target="tpu_custom_call" | custom-call | flops 469762048 | bytes 3932160 | tf_op jit(solution)/shard_map/power/pallas_call | solution.py:201
  75.8 12.5 %all_to_all.26.in_ref = f32[16,24,256]{2,1,0:T(8,128)S(1)} all-to-all(f32[16,24,256]{2,1,0:T(8,128)S(1)} %get-tuple-element.18), channel_id=1, replica_groups=mesh['expert_0'=16,'expert_1'=2,'row_0'=4,'row_1'=4] {'row_0','row_1'}, dimensions={0} | all-to-all | bytes 786432 | tf_op jit(solution)/shard_map/all_to_all | solution.py:306
  88.3 1.3 spread.3
  89.6 3.5 %all-to-all-start.3 = ((f32[16,16,256]{2,1,0:T(8,128)}), f32[16,16,256]{2,1,0:T(8,128)S(1)}, u32[]{:S(2)}, u32[]{:S(2)}) async-start(f32[16,16,256]{2,1,0:T(8,128)} %get-tuple-element.19), calls=%async_computation.3 | async-start | bytes 524288 | tf_op jit(solution)/shard_map/all_to_all | solution.py:306
  93.1 1.7 %second.1 = f32[16,256,128]{2,1,0:T(8,128)} custom-call(bf16[448,256]{1,0:T(8,128)(2,1)S(1)} %get-tuple-element.20.p_ref.left_ref, bf16[448,2048]{1,0:T(8,128)(2,1)S(1)} %bitcast.7), custom_call_target="tpu_custom_call" | custom-call | flops 469762048 | bytes 4161536 | tf_op jit(solution)/shard_map/second/pallas_call | solution.py:120
  94.9 0.0 copy-start.1
  94.9 6.9 %all-to-all-done.3.a_ref = f32[16,16,256]{2,1,0:T(8,128)S(1)} async-done(((f32[16,16,256]{2,1,0:T(8,128)}), f32[16,16,256]{2,1,0:T(8,128)S(1)}, u32[]{:S(2)}, u32[]{:S(2)}) %all-to-all-start.3) | async-done | bytes 262176 | tf_op jit(solution)/shard_map/all_to_all | solution.py:306
  101.8 3.7 %all-to-all-start.4 = ((f32[16,256,128]{2,1,0:T(8,128)}), f32[16,256,128]{2,1,0:T(8,128)S(1)}, u32[]{:S(2)}, u32[]{:S(2)}) async-start(f32[16,256,128]{2,1,0:T(8,128)} %second.1), calls=%async_computation.4 | async-start | bytes 4194304 | tf_op jit(solution)/shard_map/all_to_all | solution.py:306
  105.5 0.0 copy-done.1
  105.5 10.0 %factor.1 = (f32[256,256]{1,0:T(8,128)S(1)}, f32[448,256]{1,0:T(8,128)}) custom-call(s32[3]{0:T(128)S(1)} %add_convert_fusion.state_ref.refresh_ref, f32[16,16,256]{2,1,0:T(8,128)S(1)} %all-to-all-done.3.a_ref, bf16[448,256]{1,0:T(8,128)(2,1)S(1)} %get-tuple-element.20.p_ref.left_ref, bf16[448,256]{1,0:T(8,128)(2,1)S(1)} %bitcast.9), custom_call_target="tpu_custom_call" | custom-call | flops 6000000000 | bytes 458752 | tf_op jit(solution)/shard_map/factor/pallas_call | solution.py:271
  115.5 1.9 %collective-permute-start.1 = (f32[8,256]{1,0:T(8,128)S(1)}, f32[8,256]{1,0:T(8,128)S(1)}, u32[]{:S(2)}, u32[]{:S(2)}) collective-permute-start(f32[8,256]{1,0:T(8,128)S(1)} %slice.10), channel_id=1, source_target_pairs={{0,16},{16,0},{1,17},{17,1},{2,18},{18,2},{3,19},{19,3},{4,20},{20... | collective-permute-start | bytes 24584 | tf_op jit(solution)/shard_map/ppermute | solution.py:317
  117.5 1.1 collective-permute-done.1
  118.6 9.3 %all-to-all-done.4.parts_ref = f32[16,256,128]{2,1,0:T(8,128)S(1)} async-done(((f32[16,256,128]{2,1,0:T(8,128)}), f32[16,256,128]{2,1,0:T(8,128)S(1)}, u32[]{:S(2)}, u32[]{:S(2)}) %all-to-all-start.4) | async-done | bytes 2097184 | tf_op jit(solution)/shard_map/all_to_all | solution.py:306
  127.9 1.6 %rotate.1 = f32[256,128]{1,0:T(8,128)} custom-call(s32[3]{0:T(128)S(1)} %add_convert_fusion.state_ref.refresh_ref, f32[8,256]{1,0:T(8,128)S(1)} %add.3.sums_ref, f32[16,256,128]{2,1,0:T(8,128)S(1)} %all-to-all-done.4.parts_ref, f32[256,256]{1,0:T(8,128)S(1)} %get-tuple-element.25.inv_ref, f32[256,128]{1,0:T(8,128)S(1)} %slice.11.stale_ref), custom_call_target="tpu_custom_call" | custom-call | flops 16777216 | bytes 2097152 | tf_op jit(solution)/shard_map/rotate/pallas_call | solution.py:294
  (4 shorter events, 0.0 us)
Async XLA Ops:
  45.8 27.0 %copy-start = (bf16[1,448,2048]{2,1,0:T(8,128)(2,1)S(1)}, bf16[1,448,2048]{2,1,0:T(8,128)(2,1)}, u32[]{:S(2)}) copy-start(bf16[1,448,2048]{2,1,0:T(8,128)(2,1)} %param.4) | copy-start | bytes 5505028
  45.8 27.0 %all-to-all-start.1 = ((f32[16,256,128]{2,1,0:T(8,128)}), f32[16,256,128]{2,1,0:T(8,128)}, u32[]{:S(2)}, u32[]{:S(2)}) async-start(f32[16,256,128]{2,1,0:T(8,128)} %get-tuple-element.14), calls=%async_computation.1 | async-start | bytes 4194304 | tf_op jit(solution)/shard_map/all_to_all | solution.py:306
  50.4 0.7 collective-permute-start
  89.6 12.2 %all-to-all-start.3 = ((f32[16,16,256]{2,1,0:T(8,128)}), f32[16,16,256]{2,1,0:T(8,128)S(1)}, u32[]{:S(2)}, u32[]{:S(2)}) async-start(f32[16,16,256]{2,1,0:T(8,128)} %get-tuple-element.19), calls=%async_computation.3 | async-start | bytes 524288 | tf_op jit(solution)/shard_map/all_to_all | solution.py:306
  94.9 10.6 %copy-start.1 = (bf16[1,448,256]{2,1,0:T(8,128)(2,1)S(1)}, bf16[1,448,256]{2,1,0:T(8,128)(2,1)}, u32[]{:S(2)}) copy-start(bf16[1,448,256]{2,1,0:T(8,128)(2,1)} %param.5) | copy-start | bytes 688132
  101.8 26.1 %all-to-all-start.4 = ((f32[16,256,128]{2,1,0:T(8,128)}), f32[16,256,128]{2,1,0:T(8,128)S(1)}, u32[]{:S(2)}, u32[]{:S(2)}) async-start(f32[16,256,128]{2,1,0:T(8,128)} %second.1), calls=%async_computation.4 | async-start | bytes 4194304 | tf_op jit(solution)/shard_map/all_to_all | solution.py:306
  115.5 3.1 %collective-permute-start.1 = (f32[8,256]{1,0:T(8,128)S(1)}, f32[8,256]{1,0:T(8,128)S(1)}, u32[]{:S(2)}, u32[]{:S(2)}) collective-permute-start(f32[8,256]{1,0:T(8,128)S(1)} %slice.10), channel_id=1, source_target_pairs={{0,16},{16,0},{1,17},{17,1},{2,18},{18,2},{3,19},{19,3},{4,20},{20... | collective-permute-start | bytes 24584 | tf_op jit(solution)/shard_map/ppermute | solution.py:317

commit v3 on v2

v3 whole, which is shorter than its diff:
```python
import functools

import jax
import jax.numpy as jnp
from jax import lax
from jax.experimental import pallas as pl
from jax.experimental.pallas import tpu as pltpu
from jax.sharding import Mesh
from jax.sharding import PartitionSpec as P

ROW = ("row_0", "row_1")
EXPERT = ("expert_0", "expert_1")
F32 = jnp.float32
BF16 = jnp.bfloat16
HIGH = lax.Precision.HIGHEST
BLOCK = 32
STAGGER = 10000
NT = (((1,), (1,)), ((), ()))
TN = (((0,), (0,)), ((), ()))
VM = pl.BlockSpec(memory_space=pltpu.VMEM)
SM = pl.BlockSpec(memory_space=pltpu.SMEM)
HBM = pl.BlockSpec(memory_space=pltpu.HBM)


def cost(flops, nbytes):
    return pl.CostEstimate(flops=int(flops), bytes_accessed=int(nbytes), transcendentals=0)


def params():
    return pltpu.CompilerParams(vmem_limit_bytes=16 * 1024 * 1024)


def product_columns(lt, g_ref, i):
    return jnp.dot(lt, g_ref[:, 256 * i : 256 * (i + 1)], preferred_element_type=F32)


def put_half(both, held_ref, out_ref, sem, i, top):
    k = both.shape[0] // 2
    for h in range(2):
        block = both[:, 128 * h : 128 * (h + 1)]
        held_ref[2 * i + h, :, :128] = block[:k, :]
        held_ref[2 * i + h, :, 128:] = block[k:, :]
    copy = pltpu.make_async_copy(
        held_ref.at[pl.ds(2 * i, 2)], out_ref.at[pl.ds(2 * i, 2), pl.ds(top, k), :], sem.at[i]
    )
    copy.start()
    return copy


def first_kernel(state_ref, left_hbm, g_hbm, out_ref, left_ref, g_ref, sem):
    n = out_ref.shape[0]
    k = left_ref.shape[1]
    pairs = n // 2
    wide = pairs // 2
    left_copy = pltpu.make_async_copy(left_hbm, left_ref, sem.at[2])
    left_copy.start()
    loads = []
    for i in range(2):
        cols = pl.ds(256 * wide * i, 256 * wide)
        loads.append(pltpu.make_async_copy(g_hbm.at[:, cols], g_ref.at[:, cols], sem.at[i]))
        loads[-1].start()

    @pl.when(state_ref[2] > 0)
    def _():
        pl.delay(STAGGER)

    left_copy.wait()
    lt = left_ref[...].astype(F32).T.astype(BF16)
    squares = jnp.zeros((8, 256), F32)
    for i in range(pairs):
        if i % wide == 0:
            loads[i // wide].wait()
        both = product_columns(lt, g_ref, i)
        for h in range(2):
            out_ref[2 * i + h, :k, :] = both[:, 128 * h : 128 * (h + 1)]
        part = g_ref[:, 256 * i : 256 * (i + 1)].astype(F32)
        squares = squares + (part * part).reshape(-1, 8, 256).sum(axis=0)
    live = state_ref[1] > 0
    squares = jnp.where(live, squares[:, :128] + squares[:, 128:], 0.0)
    slot = jnp.where(live, jnp.full((8, 128), 1.0 / (8 * 128 * n), F32), 0.0)
    for j in range(n):
        out_ref[j, k : k + 8, :] = squares
        out_ref[j, k + 8 :, :] = slot


def first(state, left, g):
    d, k = left.shape
    s = g.shape[1]
    n = s // 128
    return pl.pallas_call(
        first_kernel,
        in_specs=[SM, HBM, HBM],
        out_specs=VM,
        out_shape=jax.ShapeDtypeStruct((n, k + 16, 128), F32),
        scratch_shapes=[pltpu.VMEM((d, k), BF16), pltpu.VMEM((d, s), BF16), pltpu.SemaphoreType.DMA((3,))],
        compiler_params=params(),
        cost_estimate=cost(2 * d * k * s, 2 * d * (s + k) + 4 * k * s),
        name="first",
    )(state, pltpu.with_memory_space_constraint(left, pltpu.HBM), pltpu.with_memory_space_constraint(g, pltpu.HBM))


def second_kernel(top, left_ref, g_ref, out_ref, held_ref, sem):
    lt = left_ref[...].astype(F32).T.astype(BF16)
    lt = lt[lt.shape[0] // 2 :, :]
    n = held_ref.shape[0]
    stores = [put_half(product_columns(lt, g_ref, i), held_ref, out_ref, sem, i, top) for i in range(n // 2)]
    for copy in stores:
        copy.wait()


def second(left, g):
    d, k = left.shape
    s = g.shape[1]
    n = s // 128
    top = k // n
    return pl.pallas_call(
        functools.partial(second_kernel, top),
        in_specs=[VM, VM],
        out_specs=HBM,
        out_shape=pltpu.HBM((n, top + k // 4, 256), F32),
        scratch_shapes=[pltpu.VMEM((n, k // 4, 256), F32), pltpu.SemaphoreType.DMA((n // 2,))],
        compiler_params=params(),
        cost_estimate=cost(d * k * s, 2 * d * (s + k) + 2 * k * s),
        name="second",
    )(left, g)


def share_kernel(top, in_ref, open_ref, sums_ref, half_ref, out_ref, own_ref, sem):
    n = in_ref.shape[0]
    own_ref[...] = in_ref[:, :top, :].sum(axis=0)
    copies = []
    for j in range(n):
        copies.append(pltpu.make_async_copy(own_ref, out_ref.at[j, pl.ds(0, top)], sem.at[j]))
        copies[-1].start()
    sums_ref[...] = in_ref[:, top : top + 8, :].sum(axis=0)
    half_ref[...] = in_ref[:, top + 8 :, :].sum(axis=0)
    for copy in copies:
        copy.wait()


def share(parts, opened, top):
    n, r, c = parts.shape
    return pl.pallas_call(
        functools.partial(share_kernel, top),
        in_specs=[VM, HBM],
        out_specs=[VM, VM, HBM],
        out_shape=[
            jax.ShapeDtypeStruct((8, c), F32),
            jax.ShapeDtypeStruct((r - top - 8, c), F32),
            pltpu.HBM(opened.shape, F32),
        ],
        scratch_shapes=[pltpu.VMEM((top, c), F32), pltpu.SemaphoreType.DMA((n,))],
        input_output_aliases={1: 2},
        compiler_params=params(),
        cost_estimate=cost(n * r * c, 4 * n * r * c),
        name="share",
    )(parts, opened)


def spread_kernel(in_ref, own_out, kept_ref, out_ref, own_ref, sem):
    n = in_ref.shape[0]
    rows = own_ref.shape[0]
    step = rows // 4
    copies = []
    for c in range(4):
        at = pl.ds(c * step, step)
        own_ref[at, :] = in_ref[:, at, :].sum(axis=0)
        for j in range(n):
            copies.append(pltpu.make_async_copy(own_ref.at[at], out_ref.at[j, at], sem.at[c, j]))
            copies[-1].start()
    copies.append(pltpu.make_async_copy(own_ref, own_out, sem.at[4, 0]))
    copies[-1].start()
    kept_ref[...] = in_ref[:, rows:, :].sum(axis=0)
    for copy in copies:
        copy.wait()


def spread(parts, kept):
    n, r, c = parts.shape
    return pl.pallas_call(
        spread_kernel,
        in_specs=[VM],
        out_specs=[HBM, VM, HBM],
        out_shape=[
            pltpu.HBM((r - kept, c), F32),
            jax.ShapeDtypeStruct((kept, c), F32),
            pltpu.HBM((n, r - kept, c), F32),
        ],
        scratch_shapes=[pltpu.VMEM((r - kept, c), F32), pltpu.SemaphoreType.DMA((5, n))],
        compiler_params=params(),
        cost_estimate=cost(n * r * c, 8 * n * r * c),
        name="spread",
    )(parts)


def power_of_two(m):
    s = jnp.ones_like(m)
    for e in (64, 32, 16, 8, 4, 2, 1):
        big = m >= 2.0**e
        s = jnp.where(big, s * 2.0**-e, s)
        m = jnp.where(big, m * 2.0**-e, m)
    for e in (64, 32, 16, 8, 4, 2, 1):
        small = m < 2.0 ** (1 - e)
        s = jnp.where(small, s * 2.0 ** (e - 1), s)
        m = jnp.where(small, m * 2.0 ** (e - 1), m)
    return s


def power_kernel(g_ref, w_hbm, extra_ref, p_ref, out_ref, w_ref, head_ref, held_ref, in_sem, sem):
    n, k, _ = w_ref.shape
    top = k // n
    step = n // 4
    loads = []
    for c in range(4):
        at = pl.ds(c * step, step)
        loads.append(pltpu.make_async_copy(w_hbm.at[at], w_ref.at[at], in_sem.at[c]))
        loads[-1].start()
    m = jnp.zeros(w_ref.shape[1:], F32)
    acc = jnp.zeros(p_ref.shape, F32)
    for j in range(0, n, 2):
        if j % step == 0:
            loads[j // step].wait()
        m = jnp.maximum(m, jnp.maximum(jnp.abs(w_ref[j]), jnp.abs(w_ref[j + 1])))
        w = jnp.concatenate([w_ref[j], w_ref[j + 1]], axis=1).astype(BF16)
        acc = acc + lax.dot_general(g_ref[:, 128 * j : 128 * j + 256], w, NT, preferred_element_type=F32)
    scale = power_of_two(jnp.max(m.T, axis=0, keepdims=True))
    acc = acc * scale
    p = acc.astype(BF16)
    p_ref[...] = p
    pt = p.astype(F32).T.astype(BF16)
    half = pt[: k // 2, :]
    stores = [
        put_half(product_columns(half, g_ref, i), held_ref, out_ref, sem, i, top + 8) for i in range(n // 2)
    ]
    head_ref[:, :top, :] = jnp.dot(pt, p, preferred_element_type=F32).reshape(n, top, k)
    extra = jnp.concatenate([extra_ref[:8, :], extra_ref[8:, :]], axis=1)
    for j in range(n):
        head_ref[j, top:, :] = extra
    last = pltpu.make_async_copy(head_ref, out_ref.at[:, pl.ds(0, top + 8), :], sem.at[n // 2])
    last.start()
    for copy in stores:
        copy.wait()
    last.wait()


def power(g, w, extra):
    d, s = g.shape
    n, k, _ = w.shape
    top = k // n + 8
    return pl.pallas_call(
        power_kernel,
        in_specs=[VM, HBM, VM],
        out_specs=[VM, HBM],
        out_shape=[jax.ShapeDtypeStruct((d, k), BF16), pltpu.HBM((n, top + k // 4, k), F32)],
        scratch_shapes=[
            pltpu.VMEM(w.shape, F32),
            pltpu.VMEM((n, top, k), F32),
            pltpu.VMEM((n, k // 4, k), F32),
            pltpu.SemaphoreType.DMA((4,)),
            pltpu.SemaphoreType.DMA((n // 2 + 1,)),
        ],
        compiler_params=params(),
        cost_estimate=cost(3 * d * k * s, 2 * d * s + 6 * k * s),
        name="power",
    )(g, pltpu.with_memory_space_constraint(w, pltpu.HBM), extra)


def sub(v, r):
    return jnp.broadcast_to(v[r : r + 1, :], v.shape)


def small_inverse(d):
    groups = BLOCK // 8
    row = lax.broadcasted_iota(jnp.int32, (8, 128), 0)
    lane = lax.broadcasted_iota(jnp.int32, (8, 128), 1)
    x = [jnp.where(lane == row + 8 * g, 1.0, 0.0) for g in range(groups)]
    c = [
        {g: jnp.broadcast_to(d[8 * g : 8 * g + 8, k : k + 1], (8, 128)) for g in range(k // 8, groups)}
        for k in range(BLOCK)
    ]
    for j in range(BLOCK):
        gj, sj = j // 8, j % 8
        r = lax.rsqrt(sub(c[j][gj], sj))
        low = {g: c[j][g] * r for g in range(gj, groups)}
        for k in range(j + 1, BLOCK):
            at = sub(low[k // 8], k % 8)
            for g in range(k // 8, groups):
                c[k][g] = c[k][g] - low[g] * at
        xr = sub(x[gj], sj) * r
        below = jnp.where(row > sj, low[gj], 0.0)
        x[gj] = jnp.where(row == sj, xr, x[gj] - below * xr)
        for g in range(gj + 1, groups):
            x[g] = x[g] - low[g] * xr
    return jnp.concatenate(x, axis=0)


def lower_inverse(m_ref):
    k = m_ref.shape[0]
    lane = lax.broadcasted_iota(jnp.int32, (BLOCK, k), 1)
    row = lax.broadcasted_iota(jnp.int32, (BLOCK, k), 0)
    for b in range(k // BLOCK):
        lo = b * BLOCK
        hi = lo + BLOCK
        r = m_ref[lo:hi, :]
        x = small_inverse(r[:, lo:hi])[:, :BLOCK]
        inside = jnp.logical_and(lane >= lo, lane < hi)
        r = jnp.where(inside, jnp.where(lane - lo == row, 1.0, 0.0), r)
        t = jnp.dot(x, r, precision=HIGH, preferred_element_type=F32)
        m_ref[lo:hi, :] = jnp.where(lane < hi, t, 0.0)
        for at, end in ((hi, min(hi + BLOCK, k)), (hi + BLOCK, k)):
            if at < end:
                old = m_ref[at:end, :]
                shape = old.shape
                column = lax.broadcasted_iota(jnp.int32, shape, 1)
                old = jnp.where(jnp.logical_and(column >= lo, column < hi), 0.0, old)
                m_ref[at:end, :] = old - lax.dot_general(
                    t[:, at:end], t, TN, precision=HIGH, preferred_element_type=F32
                )


def finish_kernel(size, state_ref, sums_ref, half_ref, parts_ref, stale_ref, p_ref, basis_ref, new_ref, out_ref, m_ref):
    n = parts_ref.shape[0]
    k = m_ref.shape[0]
    top = k // n
    m_ref[...] = parts_ref[:, :top, :].reshape(k, k)
    upper = half_ref[...]
    lower = parts_ref[:, top:, :].sum(axis=0)
    cross = jnp.concatenate([upper[:, :128], upper[:, 128:], lower[:, :128], lower[:, 128:]], axis=0)
    lower_inverse(m_ref)
    inv = m_ref[...]
    p = p_ref[...]
    fresh = jnp.zeros(new_ref.shape, F32)
    rest = inv
    for _ in range(3):
        piece = rest.astype(BF16)
        rest = rest - piece.astype(F32)
        fresh = fresh + lax.dot_general(p, piece, NT, preferred_element_type=F32)
    old = jnp.where(state_ref[1] > 0, basis_ref[...].astype(F32), 0.0)
    new_ref[...] = jnp.where(state_ref[0] > 0, fresh, old)
    turned = jnp.dot(inv, cross, precision=HIGH, preferred_element_type=F32)
    squares = jnp.sum(sums_ref[:, :128], axis=(0, 1), keepdims=True)
    slots = jnp.sum(sums_ref[:, 128:], axis=(0, 1), keepdims=True)
    scale = lax.rsqrt(squares / (slots * size) + 1e-06)
    stale = jnp.where(state_ref[1] > 0, stale_ref[...], 0.0)
    out_ref[...] = jnp.where(state_ref[0] > 0, turned, stale) * scale


def finish(size, state, sums, half, parts, stale, p, basis):
    d, k = p.shape
    return pl.pallas_call(
        functools.partial(finish_kernel, size),
        in_specs=[SM] + [VM] * 6,
        out_specs=[VM, VM],
        out_shape=[jax.ShapeDtypeStruct((d, k), F32), jax.ShapeDtypeStruct((k, 128), F32)],
        scratch_shapes=[pltpu.VMEM((k, k), F32)],
        compiler_params=params(),
        cost_estimate=cost(6e9, 4 * d * k),
        name="finish",
    )(state, sums, half, parts, stale, p, basis)


def exchange(blocks, axes):
    return lax.all_to_all(blocks, axes, split_axis=0, concat_axis=0, tiled=True)


def between_planes(value):
    far = lax.axis_size(EXPERT[0])
    rows = lax.axis_size(ROW)
    pairs = [(z * rows + r, (z + r) % far * rows + r) for z in range(far) for r in range(rows)]
    return lax.ppermute(value, (EXPERT[0],) + ROW, pairs)


def both_cores(value):
    return value + lax.ppermute(value, EXPERT[1], [(0, 1), (1, 0)])


def on_device(d_whole, grads, basis, loads, flags):
    g, b = grads[0], basis[0]
    k = b.shape[1]
    s = g.shape[1]
    live = loads[0] >= 1
    refresh = jnp.logical_and(live, flags[0] == 1)
    late = lax.axis_index(EXPERT[1]) == 0
    state = jnp.stack([refresh, live, late]).astype(jnp.int32)

    received = exchange(first(state, b, g), ROW)
    n = received.shape[0]
    stale, plane, copies = spread(received, 16)
    planes = between_planes(plane)
    received, planes = lax.optimization_barrier((exchange(copies, ROW), planes))
    p, sent = power(g, received, planes)
    top = k // n
    sums, half, sent = share(exchange(sent, ROW), second(p, g), top)
    received, sums = lax.optimization_barrier((exchange(sent, ROW), both_cores(sums)))
    new_basis, rotated = finish(float(d_whole * s), state, sums, half, received, stale, p, b)
    return new_basis[None], rotated[None]


def solution(mesh):
    torus = Mesh(mesh.devices.reshape(16, 2, 4, 4), EXPERT + ROW)
    placed = (P(EXPERT, ROW, None), P(EXPERT, ROW, None), P(EXPERT), P(EXPERT))

    def whole(grads, basis, loads, flags):
        return jax.shard_map(
            functools.partial(on_device, grads.shape[1]),
            mesh=torus,
            in_specs=placed,
            out_specs=(P(EXPERT, ROW, None), P(EXPERT, None, ROW)),
            check_vma=False,
        )(grads, basis, loads, flags)

    return whole
```

time: 130 us -> 125 us (0.962)
  blocking collectives: 41.5 us -> 28 us
  waiting for transfers between devices: 39 us -> 50 us
  Pallas kernels: 32.4 us -> 30 us
    all_to_all x2 -> x1, blocking collectives: 41.5 us -> 28 us  [exchange(): return lax.all_to_all(blocks, axes, split_axis=0, concat_axis=0, tiled=True)]
    all_to_all x3, waiting for transfers between devices: 37.9 us -> 48.8 us  [exchange(): return lax.all_to_all(blocks, axes, split_axis=0, concat_axis=0, tiled=True)]
    pallas_call x7 -> x6, Pallas kernels: 32.4 us -> 30 us  [the longest x1 11.6 us: first(): pl.pallas_call(first_kernel, in_specs=[SM, HBM, HBM], out_specs=VM, out_s...]
  transfers between devices with their start and end apart: 5 -> 5, of which waited for: 4 -> 4; matrix products, arithmetic and copies ran while one was open for 0% -> 0% of each run, Pallas kernels for 9% -> 1%
where the time goes in v3:
time: 125 us
  waiting for transfers between devices  50 us (40%)
  Pallas kernels  30 us (24%)
  blocking collectives  28 us (22%)
  starting transfers between devices  14.7 us (12%)
  between operations  2.05 us (2%)
    all_to_all x3, waiting for transfers between devices, exchange(): return lax.all_to_all(blocks, axes, split_axis=0, concat_axis=0, tiled=True)  48.8 us
    all_to_all x1, blocking collectives, exchange(): return lax.all_to_all(blocks, axes, split_axis=0, concat_axis=0, tiled=True)  28 us
    all_to_all x3, starting transfers between devices, exchange(): return lax.all_to_all(blocks, axes, split_axis=0, concat_axis=0, tiled=True)  12.1 us
    pallas_call x1, Pallas kernels, first(): pl.pallas_call(first_kernel, in_specs=[SM, HBM, HBM], out_specs=VM, out_s...  11.6 us
    pallas_call x1, Pallas kernels, finish(): pl.pallas_call(functools.partial(finish_kernel, size), in_specs=[SM] + [V...  9.93 us
    pallas_call x1, Pallas kernels, power(): pl.pallas_call(power_kernel, in_specs=[VM, HBM, VM], out_specs=[VM, HBM],...  4.12 us
  transfers between devices with their start and end apart: 5, of which 4 were waited for; matrix products, arithmetic and copies ran while one was open for 0% of the time, Pallas kernels for 1%

profile of v3, /device:TPU:480, one launch (start us, length us, event | category | flops | bytes accessed | tf_op | source)
XLA Modules:
  0.0 124.8 jit_solution(2753471199154114899)
XLA Ops:
  1.9 0.1 add_convert_fusion.state_ref
  2.0 11.6 %first.1 = f32[16,272,128]{2,1,0:T(8,128)S(1)} custom-call(s32[3]{0:T(128)S(1)} %add_convert_fusion.state_ref, bf16[448,256]{1,0:T(8,128)(2,1)} %bitcast.8, bf16[448,2048]{1,0:T(8,128)(2,1)} %bitcast.5), custom_call_target="tpu_custom_call" | custom-call | flops 469762048 | bytes 4161536 | tf_op jit(solution)/shard_map/first/pallas_call | solution.py:90
  13.6 28.0 %all_to_all.20.in_ref = f32[16,272,128]{2,1,0:T(8,128)S(1)} all-to-all(f32[16,272,128]{2,1,0:T(8,128)S(1)} %first.1), channel_id=1, replica_groups=mesh['expert_0'=16,'expert_1'=2,'row_0'=4,'row_1'=4] {'row_0','row_1'}, dimensions={0} | all-to-all | bytes 4456448 | tf_op jit(solution)/shard_map/all_to_all | solution.py:363
  41.6 2.1 %spread.1 = (f32[256,128]{1,0:T(8,128)}, f32[16,128]{1,0:T(8,128)S(1)}, f32[16,256,128]{2,1,0:T(8,128)}) custom-call(f32[16,272,128]{2,1,0:T(8,128)S(1)} %all_to_all.20.in_ref), custom_call_target="tpu_custom_call" | custom-call | flops 557056 | bytes 4456448 | tf_op jit(solution)/shard_map/spread/pallas_call | solution.py:180
  43.7 0.0 copy-start
  43.7 4.6 %all-to-all-start.1 = ((f32[16,256,128]{2,1,0:T(8,128)}), f32[16,256,128]{2,1,0:T(8,128)}, u32[]{:S(2)}, u32[]{:S(2)}) async-start(f32[16,256,128]{2,1,0:T(8,128)} %get-tuple-element.16), calls=%async_computation.1 | async-start | bytes 4194304 | tf_op jit(solution)/shard_map/all_to_all | solution.py:363
  48.3 0.7 collective-permute-start
  49.0 0.0 collective-permute-done.extra_ref
  49.0 21.7 %all-to-all-done.1.w_hbm = f32[16,256,128]{2,1,0:T(8,128)} async-done(((f32[16,256,128]{2,1,0:T(8,128)}), f32[16,256,128]{2,1,0:T(8,128)}, u32[]{:S(2)}, u32[]{:S(2)}) %all-to-all-start.1) | async-done | bytes 2097184 | tf_op jit(solution)/shard_map/all_to_all | solution.py:363
  70.7 0.0 copy-done
  70.7 4.1 %power.1 = (bf16[448,256]{1,0:T(8,128)(2,1)S(1)}, f32[16,88,256]{2,1,0:T(8,128)}) custom-call(bf16[448,2048]{1,0:T(8,128)(2,1)S(1)} %bitcast.6, f32[16,256,128]{2,1,0:T(8,128)} %all-to-all-done.1.w_hbm, f32[16,128]{1,0:T(8,128)S(1)} %collective-permute-done.extra_ref), custom_call_target="tpu_custom_call" | custom-call | flops 704643072 | bytes 4980736 | tf_op jit(solution)/shard_map/power/pallas_call | solution.py:250
  74.8 3.7 %all-to-all-start.2 = ((f32[16,88,256]{2,1,0:T(8,128)}), f32[16,88,256]{2,1,0:T(8,128)S(1)}, u32[]{:S(2)}, u32[]{:S(2)}) async-start(f32[16,88,256]{2,1,0:T(8,128)} %get-tuple-element.20), calls=%async_computation.2 | async-start | bytes 2883584 | tf_op jit(solution)/shard_map/all_to_all | solution.py:363
  78.5 1.4 %second.1.open_ref = f32[16,80,256]{2,1,0:T(8,128)} custom-call(bf16[448,256]{1,0:T(8,128)(2,1)S(1)} %get-tuple-element.21.left_ref.p_ref, bf16[448,2048]{1,0:T(8,128)(2,1)S(1)} %bitcast.7), custom_call_target="tpu_custom_call" | custom-call | flops 234881024 | bytes 3112960 | tf_op jit(solution)/shard_map/second/pallas_call | solution.py:116
  79.9 15.0 %all-to-all-done.2.in_ref = f32[16,88,256]{2,1,0:T(8,128)S(1)} async-done(((f32[16,88,256]{2,1,0:T(8,128)}), f32[16,88,256]{2,1,0:T(8,128)S(1)}, u32[]{:S(2)}, u32[]{:S(2)}) %all-to-all-start.2) | async-done | bytes 1441824 | tf_op jit(solution)/shard_map/all_to_all | solution.py:363
  94.9 0.9 share.1
  95.8 0.0 copy-start.1
  95.8 0.0 copy-start.2
  95.8 3.8 %all-to-all-start.3 = ((f32[16,80,256]{2,1,0:T(8,128)}), f32[16,80,256]{2,1,0:T(8,128)S(1)}, u32[]{:S(2)}, u32[]{:S(2)}) async-start(f32[16,80,256]{2,1,0:T(8,128)} %get-tuple-element.22), calls=%async_computation.3 | async-start | bytes 2621440 | tf_op jit(solution)/shard_map/all_to_all | solution.py:363
  99.7 1.9 %collective-permute-start.1 = (f32[8,256]{1,0:T(8,128)S(1)}, f32[8,256]{1,0:T(8,128)S(1)}, u32[]{:S(2)}, u32[]{:S(2)}) collective-permute-start(f32[8,256]{1,0:T(8,128)S(1)} %get-tuple-element.23), channel_id=1, source_target_pairs={{0,16},{16,0},{1,17},{17,1},{2,18},{18,2},{3,19},{19,3},{4,20},{20... | collective-permute-start | bytes 24584 | tf_op jit(solution)/shard_map/ppermute | solution.py:374
  101.6 1.1 collective-permute-done.1
  102.7 12.1 %all-to-all-done.3.parts_ref = f32[16,80,256]{2,1,0:T(8,128)S(1)} async-done(((f32[16,80,256]{2,1,0:T(8,128)}), f32[16,80,256]{2,1,0:T(8,128)S(1)}, u32[]{:S(2)}, u32[]{:S(2)}) %all-to-all-start.3) | async-done | bytes 1310752 | tf_op jit(solution)/shard_map/all_to_all | solution.py:363
  114.9 0.0 copy-done.1
  114.9 0.0 copy-done.2
  114.9 9.9 %finish.1 = (f32[448,256]{1,0:T(8,128)}, f32[256,128]{1,0:T(8,128)}) custom-call(s32[3]{0:T(128)S(1)} %add_convert_fusion.state_ref, f32[8,256]{1,0:T(8,128)S(1)} %add.3.sums_ref, f32[64,256]{1,0:T(8,128)S(1)} %get-tuple-element.25.half_ref, f32[16,80,256]{2,1,0:T(8,128)S(1)} %all-to-all-done.3.parts_ref, f32[256,128]{1,0:T(8,128)S(1)} %copy-done.2, ...), custom_call_target="tpu_custom_call" | custom-call | flops 6000000000 | bytes 458752 | tf_op jit(solution)/shard_map/finish/pallas_call | solution.py:350
  (1 shorter events, 0.0 us)
Async XLA Ops:
  43.7 27.0 %copy-start = (bf16[1,448,2048]{2,1,0:T(8,128)(2,1)S(1)}, bf16[1,448,2048]{2,1,0:T(8,128)(2,1)}, u32[]{:S(2)}) copy-start(bf16[1,448,2048]{2,1,0:T(8,128)(2,1)} %param.4) | copy-start | bytes 5505028
  43.7 27.0 %all-to-all-start.1 = ((f32[16,256,128]{2,1,0:T(8,128)}), f32[16,256,128]{2,1,0:T(8,128)}, u32[]{:S(2)}, u32[]{:S(2)}) async-start(f32[16,256,128]{2,1,0:T(8,128)} %get-tuple-element.16), calls=%async_computation.1 | async-start | bytes 4194304 | tf_op jit(solution)/shard_map/all_to_all | solution.py:363
  48.3 0.7 collective-permute-start
  74.8 20.1 %all-to-all-start.2 = ((f32[16,88,256]{2,1,0:T(8,128)}), f32[16,88,256]{2,1,0:T(8,128)S(1)}, u32[]{:S(2)}, u32[]{:S(2)}) async-start(f32[16,88,256]{2,1,0:T(8,128)} %get-tuple-element.20), calls=%async_computation.2 | async-start | bytes 2883584 | tf_op jit(solution)/shard_map/all_to_all | solution.py:363
  95.8 19.1 %copy-start.1 = (bf16[1,448,256]{2,1,0:T(8,128)(2,1)S(1)}, bf16[1,448,256]{2,1,0:T(8,128)(2,1)}, u32[]{:S(2)}) copy-start(bf16[1,448,256]{2,1,0:T(8,128)(2,1)} %param.5) | copy-start | bytes 688132
  95.8 19.0 %copy-start.2 = (f32[256,128]{1,0:T(8,128)S(1)}, f32[256,128]{1,0:T(8,128)}, u32[]{:S(2)}) copy-start(f32[256,128]{1,0:T(8,128)} %get-tuple-element.27.stale_ref) | copy-start | bytes 393220
  95.8 19.0 %all-to-all-start.3 = ((f32[16,80,256]{2,1,0:T(8,128)}), f32[16,80,256]{2,1,0:T(8,128)S(1)}, u32[]{:S(2)}, u32[]{:S(2)}) async-start(f32[16,80,256]{2,1,0:T(8,128)} %get-tuple-element.22), calls=%async_computation.3 | async-start | bytes 2621440 | tf_op jit(solution)/shard_map/all_to_all | solution.py:363
  99.7 3.1 %collective-permute-start.1 = (f32[8,256]{1,0:T(8,128)S(1)}, f32[8,256]{1,0:T(8,128)S(1)}, u32[]{:S(2)}, u32[]{:S(2)}) collective-permute-start(f32[8,256]{1,0:T(8,128)S(1)} %get-tuple-element.23), channel_id=1, source_target_pairs={{0,16},{16,0},{1,17},{17,1},{2,18},{18,2},{3,19},{19,3},{4,20},{20... | collective-permute-start | bytes 24584 | tf_op jit(solution)/shard_map/ppermute | solution.py:374

commit v4 on v3

--- a/solution.py
+++ b/solution.py
@@ -34,17 +34,12 @@
     return jnp.dot(lt, g_ref[:, 256 * i : 256 * (i + 1)], preferred_element_type=F32)
 
 
-def put_half(both, held_ref, out_ref, sem, i, top):
+def put_half(both, out_ref, i, top):
     k = both.shape[0] // 2
     for h in range(2):
         block = both[:, 128 * h : 128 * (h + 1)]
-        held_ref[2 * i + h, :, :128] = block[:k, :]
-        held_ref[2 * i + h, :, 128:] = block[k:, :]
-    copy = pltpu.make_async_copy(
-        held_ref.at[pl.ds(2 * i, 2)], out_ref.at[pl.ds(2 * i, 2), pl.ds(top, k), :], sem.at[i]
-    )
-    copy.start()
-    return copy
+        out_ref[2 * i + h, top : top + k, :128] = block[:k, :]
+        out_ref[2 * i + h, top : top + k, 128:] = block[k:, :]
 
 
 def first_kernel(state_ref, left_hbm, g_hbm, out_ref, left_ref, g_ref, sem):
@@ -76,11 +71,12 @@
         part = g_ref[:, 256 * i : 256 * (i + 1)].astype(F32)
         squares = squares + (part * part).reshape(-1, 8, 256).sum(axis=0)
     live = state_ref[1] > 0
-    squares = jnp.where(live, squares[:, :128] + squares[:, 128:], 0.0)
-    slot = jnp.where(live, jnp.full((8, 128), 1.0 / (8 * 128 * n), F32), 0.0)
+    squares = squares[:, :128] + squares[:, 128:]
+    squares = jnp.where(live, squares[:4, :] + squares[4:, :], 0.0)
+    slot = jnp.where(live, jnp.full((4, 128), 1.0 / (4 * 128 * n), F32), 0.0)
+    extra = jnp.concatenate([squares, slot], axis=0)
     for j in range(n):
-        out_ref[j, k : k + 8, :] = squares
-        out_ref[j, k + 8 :, :] = slot
+        out_ref[j, k:, :] = extra
 
 
 def first(state, left, g):
@@ -91,7 +87,7 @@
         first_kernel,
         in_specs=[SM, HBM, HBM],
         out_specs=VM,
-        out_shape=jax.ShapeDtypeStruct((n, k + 16, 128), F32),
+        out_shape=jax.ShapeDtypeStruct((n, k + 8, 128), F32),
         scratch_shapes=[pltpu.VMEM((d, k), BF16), pltpu.VMEM((d, s), BF16), pltpu.SemaphoreType.DMA((3,))],
         compiler_params=params(),
         cost_estimate=cost(2 * d * k * s, 2 * d * (s + k) + 4 * k * s),
@@ -99,62 +95,37 @@
     )(state, pltpu.with_memory_space_constraint(left, pltpu.HBM), pltpu.with_memory_space_constraint(g, pltpu.HBM))
 
 
-def second_kernel(top, left_ref, g_ref, out_ref, held_ref, sem):
-    lt = left_ref[...].astype(F32).T.astype(BF16)
-    lt = lt[lt.shape[0] // 2 :, :]
-    n = held_ref.shape[0]
-    stores = [put_half(product_columns(lt, g_ref, i), held_ref, out_ref, sem, i, top) for i in range(n // 2)]
-    for copy in stores:
-        copy.wait()
-
-
-def second(left, g):
-    d, k = left.shape
-    s = g.shape[1]
-    n = s // 128
-    top = k // n
-    return pl.pallas_call(
-        functools.partial(second_kernel, top),
-        in_specs=[VM, VM],
-        out_specs=HBM,
-        out_shape=pltpu.HBM((n, top + k // 4, 256), F32),
-        scratch_shapes=[pltpu.VMEM((n, k // 4, 256), F32), pltpu.SemaphoreType.DMA((n // 2,))],
-        compiler_params=params(),
-        cost_estimate=cost(d * k * s, 2 * d * (s + k) + 2 * k * s),
-        name="second",
-    )(left, g)
-
-
-def share_kernel(top, in_ref, open_ref, sums_ref, half_ref, out_ref, own_ref, sem):
+def share_kernel(top, in_ref, rest_ref, sums_ref, half_ref, out_ref, own_ref, sem):
     n = in_ref.shape[0]
+    copies = [pltpu.make_async_copy(rest_ref, out_ref.at[:, pl.ds(top, rest_ref.shape[1]), :], sem.at[n])]
+    copies[-1].start()
     own_ref[...] = in_ref[:, :top, :].sum(axis=0)
-    copies = []
     for j in range(n):
         copies.append(pltpu.make_async_copy(own_ref, out_ref.at[j, pl.ds(0, top)], sem.at[j]))
         copies[-1].start()
-    sums_ref[...] = in_ref[:, top : top + 8, :].sum(axis=0)
+    sums_ref[...] = in_ref[:, top : top + 8, :128].sum(axis=0)
     half_ref[...] = in_ref[:, top + 8 :, :].sum(axis=0)
     for copy in copies:
         copy.wait()
 
 
-def share(parts, opened, top):
+def share(parts, rest, top):
     n, r, c = parts.shape
+    below = rest.shape[1]
     return pl.pallas_call(
         functools.partial(share_kernel, top),
-        in_specs=[VM, HBM],
+        in_specs=[VM, VM],
         out_specs=[VM, VM, HBM],
         out_shape=[
-            jax.ShapeDtypeStruct((8, c), F32),
+            jax.ShapeDtypeStruct((8, 128), F32),
             jax.ShapeDtypeStruct((r - top - 8, c), F32),
-            pltpu.HBM(opened.shape, F32),
+            pltpu.HBM((n, top + below, c), F32),
         ],
-        scratch_shapes=[pltpu.VMEM((top, c), F32), pltpu.SemaphoreType.DMA((n,))],
-        input_output_aliases={1: 2},
+        scratch_shapes=[pltpu.VMEM((top, c), F32), pltpu.SemaphoreType.DMA((n + 1,))],
         compiler_params=params(),
         cost_estimate=cost(n * r * c, 4 * n * r * c),
         name="share",
-    )(parts, opened)
+    )(parts, rest)
 
 
 def spread_kernel(in_ref, own_out, kept_ref, out_ref, own_ref, sem):
@@ -206,7 +177,7 @@
     return s
 
 
-def power_kernel(g_ref, w_hbm, extra_ref, p_ref, out_ref, w_ref, head_ref, held_ref, in_sem, sem):
+def power_kernel(g_ref, w_hbm, extra_ref, p_ref, out_ref, rest_ref, w_ref, in_sem):
     n, k, _ = w_ref.shape
     top = k // n
     step = n // 4
@@ -228,39 +199,31 @@
     p = acc.astype(BF16)
     p_ref[...] = p
     pt = p.astype(F32).T.astype(BF16)
-    half = pt[: k // 2, :]
-    stores = [
-        put_half(product_columns(half, g_ref, i), held_ref, out_ref, sem, i, top + 8) for i in range(n // 2)
-    ]
-    head_ref[:, :top, :] = jnp.dot(pt, p, preferred_element_type=F32).reshape(n, top, k)
-    extra = jnp.concatenate([extra_ref[:8, :], extra_ref[8:, :]], axis=1)
+    out_ref[:, :top, :] = jnp.dot(pt, p, preferred_element_type=F32).reshape(n, top, k)
+    extra = jnp.concatenate([extra_ref[...], jnp.zeros((8, k - 128), F32)], axis=1)
     for j in range(n):
-        head_ref[j, top:, :] = extra
-    last = pltpu.make_async_copy(head_ref, out_ref.at[:, pl.ds(0, top + 8), :], sem.at[n // 2])
-    last.start()
-    for copy in stores:
-        copy.wait()
-    last.wait()
+        out_ref[j, top : top + 8, :] = extra
+    for i in range(n // 2):
+        both = product_columns(pt, g_ref, i)
+        put_half(both[: k // 2, :], out_ref, i, top + 8)
+        put_half(both[k // 2 :, :], rest_ref, i, 0)
 
 
 def power(g, w, extra):
     d, s = g.shape
     n, k, _ = w.shape
-    top = k // n + 8
     return pl.pallas_call(
         power_kernel,
         in_specs=[VM, HBM, VM],
-        out_specs=[VM, HBM],
-        out_shape=[jax.ShapeDtypeStruct((d, k), BF16), pltpu.HBM((n, top + k // 4, k), F32)],
-        scratch_shapes=[
-            pltpu.VMEM(w.shape, F32),
-            pltpu.VMEM((n, top, k), F32),
-            pltpu.VMEM((n, k // 4, k), F32),
-            pltpu.SemaphoreType.DMA((4,)),
-            pltpu.SemaphoreType.DMA((n // 2 + 1,)),
+        out_specs=[VM, VM, VM],
+        out_shape=[
+            jax.ShapeDtypeStruct((d, k), BF16),
+            jax.ShapeDtypeStruct((n, k // n + 8 + k // 4, k), F32),
+            jax.ShapeDtypeStruct((n, k // 4, k), F32),
         ],
-        compiler_params=params(),
-        cost_estimate=cost(3 * d * k * s, 2 * d * s + 6 * k * s),
+        scratch_shapes=[pltpu.VMEM(w.shape, F32), pltpu.SemaphoreType.DMA((4,))],
+        compiler_params=params(),
+        cost_estimate=cost(4 * d * k * s, 2 * d * s + 8 * k * s),
         name="power",
     )(g, pltpu.with_memory_space_constraint(w, pltpu.HBM), extra)
 
@@ -338,8 +301,8 @@
     old = jnp.where(state_ref[1] > 0, basis_ref[...].astype(F32), 0.0)
     new_ref[...] = jnp.where(state_ref[0] > 0, fresh, old)
     turned = jnp.dot(inv, cross, precision=HIGH, preferred_element_type=F32)
-    squares = jnp.sum(sums_ref[:, :128], axis=(0, 1), keepdims=True)
-    slots = jnp.sum(sums_ref[:, 128:], axis=(0, 1), keepdims=True)
+    squares = jnp.sum(sums_ref[:4, :], axis=(0, 1), keepdims=True)
+    slots = jnp.sum(sums_ref[4:, :], axis=(0, 1), keepdims=True)
     scale = lax.rsqrt(squares / (slots * size) + 1e-06)
     stale = jnp.where(state_ref[1] > 0, stale_ref[...], 0.0)
     out_ref[...] = jnp.where(state_ref[0] > 0, turned, stale) * scale
@@ -385,12 +348,12 @@
 
     received = exchange(first(state, b, g), ROW)
     n = received.shape[0]
-    stale, plane, copies = spread(received, 16)
+    stale, plane, copies = spread(received, 8)
     planes = between_planes(plane)
     received, planes = lax.optimization_barrier((exchange(copies, ROW), planes))
-    p, sent = power(g, received, planes)
+    p, sent, rest = power(g, received, planes)
     top = k // n
-    sums, half, sent = share(exchange(sent, ROW), second(p, g), top)
+    sums, half, sent = share(exchange(sent, ROW), rest, top)
     received, sums = lax.optimization_barrier((exchange(sent, ROW), both_cores(sums)))
     new_basis, rotated = finish(float(d_whole * s), state, sums, half, received, stale, p, b)
     return new_basis[None], rotated[None]

time: 125 us -> 122 us (0.976)
  blocking collectives: 28 us -> 45.1 us
  waiting for transfers between devices: 50 us -> 35 us
  starting transfers between devices: 14.7 us -> 11 us
  Pallas kernels: 30 us -> 28.5 us
    all_to_all x1 -> x2, blocking collectives: 28 us -> 45.1 us  [exchange(): return lax.all_to_all(blocks, axes, split_axis=0, concat_axis=0, tiled=True)]
    all_to_all x3 -> x2, waiting for transfers between devices: 48.8 us -> 33.8 us  [exchange(): return lax.all_to_all(blocks, axes, split_axis=0, concat_axis=0, tiled=True)]
    all_to_all x3 -> x2, starting transfers between devices: 12.1 us -> 8.43 us  [exchange(): return lax.all_to_all(blocks, axes, split_axis=0, concat_axis=0, tiled=True)]
    pallas_call x3 -> x2, Pallas kernels: 6.37 us -> 4.9 us  [the longest x1 3.67 us: power(): pl.pallas_call(power_kernel, in_specs=[VM, HBM, VM], out_specs=[VM, VM, V...]
  transfers between devices with their start and end apart: 5 -> 4, of which waited for: 4 -> 3; matrix products, arithmetic and copies ran while one was open for 0% -> 0% of each run, Pallas kernels for 1% -> 0%
where the time goes in v4:
time: 122 us
  blocking collectives  45.1 us (37%)
  waiting for transfers between devices  35 us (29%)
  Pallas kernels  28.5 us (23%)
  starting transfers between devices  11 us (9%)
  between operations  2.03 us (2%)
    all_to_all x2, blocking collectives, exchange(): return lax.all_to_all(blocks, axes, split_axis=0, concat_axis=0, tiled=True)  45.1 us
    all_to_all x2, waiting for transfers between devices, exchange(): return lax.all_to_all(blocks, axes, split_axis=0, concat_axis=0, tiled=True)  33.8 us
    pallas_call x1, Pallas kernels, first(): pl.pallas_call(first_kernel, in_specs=[SM, HBM, HBM], out_specs=VM, out_s...  11.6 us
    pallas_call x1, Pallas kernels, finish(): pl.pallas_call(functools.partial(finish_kernel, size), in_specs=[SM] + [V...  9.93 us
    all_to_all x2, starting transfers between devices, exchange(): return lax.all_to_all(blocks, axes, split_axis=0, concat_axis=0, tiled=True)  8.43 us
    pallas_call x1, Pallas kernels, power(): pl.pallas_call(power_kernel, in_specs=[VM, HBM, VM], out_specs=[VM, VM, V...  3.67 us
  transfers between devices with their start and end apart: 4, of which 3 were waited for; matrix products, arithmetic and copies ran while one was open for 0% of the time, Pallas kernels for 0%

profile of v4, /device:TPU:480, one launch (start us, length us, event | category | flops | bytes accessed | tf_op | source)
XLA Modules:
  0.0 121.7 jit_solution(2405961959459744714)
XLA Ops:
  1.9 0.1 add_convert_fusion.state_ref
  2.0 11.6 %first.1 = f32[16,264,128]{2,1,0:T(8,128)S(1)} custom-call(s32[3]{0:T(128)S(1)} %add_convert_fusion.state_ref, bf16[448,256]{1,0:T(8,128)(2,1)} %bitcast.7, bf16[448,2048]{1,0:T(8,128)(2,1)} %bitcast.5), custom_call_target="tpu_custom_call" | custom-call | flops 469762048 | bytes 4161536 | tf_op jit(solution)/shard_map/first/pallas_call | solution.py:86
  13.6 27.3 %all_to_all.20.in_ref = f32[16,264,128]{2,1,0:T(8,128)S(1)} all-to-all(f32[16,264,128]{2,1,0:T(8,128)S(1)} %first.1), channel_id=1, replica_groups=mesh['expert_0'=16,'expert_1'=2,'row_0'=4,'row_1'=4] {'row_0','row_1'}, dimensions={0} | all-to-all | bytes 4325376 | tf_op jit(solution)/shard_map/all_to_all | solution.py:326
  40.9 2.1 %spread.1 = (f32[256,128]{1,0:T(8,128)}, f32[8,128]{1,0:T(8,128)S(1)}, f32[16,256,128]{2,1,0:T(8,128)}) custom-call(f32[16,264,128]{2,1,0:T(8,128)S(1)} %all_to_all.20.in_ref), custom_call_target="tpu_custom_call" | custom-call | flops 540672 | bytes 4325376 | tf_op jit(solution)/shard_map/spread/pallas_call | solution.py:151
  43.1 0.0 copy-start
  43.1 4.6 %all-to-all-start.1 = ((f32[16,256,128]{2,1,0:T(8,128)}), f32[16,256,128]{2,1,0:T(8,128)}, u32[]{:S(2)}, u32[]{:S(2)}) async-start(f32[16,256,128]{2,1,0:T(8,128)} %get-tuple-element.17), calls=%async_computation.1 | async-start | bytes 4194304 | tf_op jit(solution)/shard_map/all_to_all | solution.py:326
  47.7 0.7 collective-permute-start
  48.3 0.0 collective-permute-done.extra_ref
  48.3 21.7 %all-to-all-done.1.w_hbm = f32[16,256,128]{2,1,0:T(8,128)} async-done(((f32[16,256,128]{2,1,0:T(8,128)}), f32[16,256,128]{2,1,0:T(8,128)}, u32[]{:S(2)}, u32[]{:S(2)}) %all-to-all-start.1) | async-done | bytes 2097184 | tf_op jit(solution)/shard_map/all_to_all | solution.py:326
  70.0 0.0 copy-done
  70.0 3.7 %power.1 = (bf16[448,256]{1,0:T(8,128)(2,1)S(1)}, f32[16,88,256]{2,1,0:T(8,128)S(1)}, f32[16,64,256]{2,1,0:T(8,128)S(1)}) custom-call(bf16[448,2048]{1,0:T(8,128)(2,1)S(1)} %bitcast.6, f32[16,256,128]{2,1,0:T(8,128)} %all-to-all-done.1.w_hbm, f32[8,128]{1,0:T(8,128)S(1)} %collective-permute-done.extra_ref), custom_call_target="tpu_custom_call" | custom-call | flops 939524096 | bytes 6029312 | tf_op jit(solution)/shard_map/power/pallas_call | solution.py:215
  73.7 17.8 %all_to_all.21.in_ref = f32[16,88,256]{2,1,0:T(8,128)S(1)} all-to-all(f32[16,88,256]{2,1,0:T(8,128)S(1)} %get-tuple-element.21), channel_id=1, replica_groups=mesh['expert_0'=16,'expert_1'=2,'row_0'=4,'row_1'=4] {'row_0','row_1'}, dimensions={0} | all-to-all | bytes 2883584 | tf_op jit(solution)/shard_map/all_to_all | solution.py:326
  91.5 1.2 %share.1 = (f32[8,128]{1,0:T(8,128)S(1)}, f32[64,256]{1,0:T(8,128)S(1)}, f32[16,80,256]{2,1,0:T(8,128)}) custom-call(f32[16,88,256]{2,1,0:T(8,128)S(1)} %all_to_all.21.in_ref, f32[16,64,256]{2,1,0:T(8,128)S(1)} %get-tuple-element.22.rest_ref), custom_call_target="tpu_custom_call" | custom-call | flops 360448 | bytes 1441792 | tf_op jit(solution)/shard_map/share/pallas_call | solution.py:115
  92.7 0.0 copy-start.1
  92.8 0.0 copy-start.2
  92.8 3.8 %all-to-all-start.3 = ((f32[16,80,256]{2,1,0:T(8,128)}), f32[16,80,256]{2,1,0:T(8,128)S(1)}, u32[]{:S(2)}, u32[]{:S(2)}) async-start(f32[16,80,256]{2,1,0:T(8,128)} %get-tuple-element.23), calls=%async_computation.3 | async-start | bytes 2621440 | tf_op jit(solution)/shard_map/all_to_all | solution.py:326
  96.6 1.9 %collective-permute-start.1 = (f32[8,128]{1,0:T(8,128)S(1)}, f32[8,128]{1,0:T(8,128)S(1)}, u32[]{:S(2)}, u32[]{:S(2)}) collective-permute-start(f32[8,128]{1,0:T(8,128)S(1)} %get-tuple-element.24), channel_id=1, source_target_pairs={{0,16},{16,0},{1,17},{17,1},{2,18},{18,2},{3,19},{19,3},{4,20},{20... | collective-permute-start | bytes 12296 | tf_op jit(solution)/shard_map/ppermute | solution.py:337
  98.5 1.1 collective-permute-done.1
  99.7 12.1 %all-to-all-done.3.parts_ref = f32[16,80,256]{2,1,0:T(8,128)S(1)} async-done(((f32[16,80,256]{2,1,0:T(8,128)}), f32[16,80,256]{2,1,0:T(8,128)S(1)}, u32[]{:S(2)}, u32[]{:S(2)}) %all-to-all-start.3) | async-done | bytes 1310752 | tf_op jit(solution)/shard_map/all_to_all | solution.py:326
  111.8 0.0 copy-done.1
  111.8 0.0 copy-done.2
  111.8 9.9 %finish.1 = (f32[448,256]{1,0:T(8,128)}, f32[256,128]{1,0:T(8,128)}) custom-call(s32[3]{0:T(128)S(1)} %add_convert_fusion.state_ref, f32[8,128]{1,0:T(8,128)S(1)} %add.3.sums_ref, f32[64,256]{1,0:T(8,128)S(1)} %get-tuple-element.26.half_ref, f32[16,80,256]{2,1,0:T(8,128)S(1)} %all-to-all-done.3.parts_ref, f32[256,128]{1,0:T(8,128)S(1)} %copy-done.2, ...), custom_call_target="tpu_custom_call" | custom-call | flops 6000000000 | bytes 458752 | tf_op jit(solution)/shard_map/finish/pallas_call | solution.py:313
  (1 shorter events, 0.0 us)
Async XLA Ops:
  43.1 27.0 %copy-start = (bf16[1,448,2048]{2,1,0:T(8,128)(2,1)S(1)}, bf16[1,448,2048]{2,1,0:T(8,128)(2,1)}, u32[]{:S(2)}) copy-start(bf16[1,448,2048]{2,1,0:T(8,128)(2,1)} %param.4) | copy-start | bytes 5505028
  43.1 27.0 %all-to-all-start.1 = ((f32[16,256,128]{2,1,0:T(8,128)}), f32[16,256,128]{2,1,0:T(8,128)}, u32[]{:S(2)}, u32[]{:S(2)}) async-start(f32[16,256,128]{2,1,0:T(8,128)} %get-tuple-element.17), calls=%async_computation.1 | async-start | bytes 4194304 | tf_op jit(solution)/shard_map/all_to_all | solution.py:326
  47.7 0.7 collective-permute-start
  92.7 19.1 %copy-start.1 = (bf16[1,448,256]{2,1,0:T(8,128)(2,1)S(1)}, bf16[1,448,256]{2,1,0:T(8,128)(2,1)}, u32[]{:S(2)}) copy-start(bf16[1,448,256]{2,1,0:T(8,128)(2,1)} %param.5) | copy-start | bytes 688132
  92.8 19.0 %copy-start.2 = (f32[256,128]{1,0:T(8,128)S(1)}, f32[256,128]{1,0:T(8,128)}, u32[]{:S(2)}) copy-start(f32[256,128]{1,0:T(8,128)} %get-tuple-element.28.stale_ref) | copy-start | bytes 393220
  92.8 19.0 %all-to-all-start.3 = ((f32[16,80,256]{2,1,0:T(8,128)}), f32[16,80,256]{2,1,0:T(8,128)S(1)}, u32[]{:S(2)}, u32[]{:S(2)}) async-start(f32[16,80,256]{2,1,0:T(8,128)} %get-tuple-element.23), calls=%async_computation.3 | async-start | bytes 2621440 | tf_op jit(solution)/shard_map/all_to_all | solution.py:326
  96.6 3.1 %collective-permute-start.1 = (f32[8,128]{1,0:T(8,128)S(1)}, f32[8,128]{1,0:T(8,128)S(1)}, u32[]{:S(2)}, u32[]{:S(2)}) collective-permute-start(f32[8,128]{1,0:T(8,128)S(1)} %get-tuple-element.24), channel_id=1, source_target_pairs={{0,16},{16,0},{1,17},{17,1},{2,18},{18,2},{3,19},{19,3},{4,20},{20... | collective-permute-start | bytes 12296 | tf_op jit(solution)/shard_map/ppermute | solution.py:337

commit v5 on v4

--- a/solution.py
+++ b/solution.py
@@ -95,14 +95,13 @@
     )(state, pltpu.with_memory_space_constraint(left, pltpu.HBM), pltpu.with_memory_space_constraint(g, pltpu.HBM))
 
 
-def share_kernel(top, in_ref, rest_ref, sums_ref, half_ref, out_ref, own_ref, sem):
-    n = in_ref.shape[0]
-    copies = [pltpu.make_async_copy(rest_ref, out_ref.at[:, pl.ds(top, rest_ref.shape[1]), :], sem.at[n])]
+def share_kernel(top, in_ref, rest_ref, sums_ref, half_ref, out_ref, wide_ref, sem):
+    copies = [pltpu.make_async_copy(rest_ref, out_ref.at[:, pl.ds(top, rest_ref.shape[1]), :], sem.at[1])]
     copies[-1].start()
-    own_ref[...] = in_ref[:, :top, :].sum(axis=0)
-    for j in range(n):
-        copies.append(pltpu.make_async_copy(own_ref, out_ref.at[j, pl.ds(0, top)], sem.at[j]))
-        copies[-1].start()
+    total = in_ref[:, :top, :].sum(axis=0)
+    wide_ref[...] = jnp.broadcast_to(total[None], wide_ref.shape)
+    copies.append(pltpu.make_async_copy(wide_ref, out_ref.at[:, pl.ds(0, top), :], sem.at[0]))
+    copies[-1].start()
     sums_ref[...] = in_ref[:, top : top + 8, :128].sum(axis=0)
     half_ref[...] = in_ref[:, top + 8 :, :].sum(axis=0)
     for copy in copies:
@@ -121,25 +120,25 @@
             jax.ShapeDtypeStruct((r - top - 8, c), F32),
             pltpu.HBM((n, top + below, c), F32),
         ],
-        scratch_shapes=[pltpu.VMEM((top, c), F32), pltpu.SemaphoreType.DMA((n + 1,))],
+        scratch_shapes=[pltpu.VMEM((n, top, c), F32), pltpu.SemaphoreType.DMA((2,))],
         compiler_params=params(),
         cost_estimate=cost(n * r * c, 4 * n * r * c),
         name="share",
     )(parts, rest)
 
 
-def spread_kernel(in_ref, own_out, kept_ref, out_ref, own_ref, sem):
-    n = in_ref.shape[0]
+def spread_kernel(in_ref, own_out, kept_ref, out_ref, own_ref, wide_ref, sem):
     rows = own_ref.shape[0]
     step = rows // 4
     copies = []
     for c in range(4):
         at = pl.ds(c * step, step)
-        own_ref[at, :] = in_ref[:, at, :].sum(axis=0)
-        for j in range(n):
-            copies.append(pltpu.make_async_copy(own_ref.at[at], out_ref.at[j, at], sem.at[c, j]))
-            copies[-1].start()
-    copies.append(pltpu.make_async_copy(own_ref, own_out, sem.at[4, 0]))
+        total = in_ref[:, at, :].sum(axis=0)
+        own_ref[at, :] = total
+        wide_ref[:, at, :] = jnp.broadcast_to(total[None], (wide_ref.shape[0], *total.shape))
+        copies.append(pltpu.make_async_copy(wide_ref.at[:, at], out_ref.at[:, at], sem.at[c]))
+        copies[-1].start()
+    copies.append(pltpu.make_async_copy(own_ref, own_out, sem.at[4]))
     copies[-1].start()
     kept_ref[...] = in_ref[:, rows:, :].sum(axis=0)
     for copy in copies:
@@ -157,7 +156,11 @@
             jax.ShapeDtypeStruct((kept, c), F32),
             pltpu.HBM((n, r - kept, c), F32),
         ],
-        scratch_shapes=[pltpu.VMEM((r - kept, c), F32), pltpu.SemaphoreType.DMA((5, n))],
+        scratch_shapes=[
+            pltpu.VMEM((r - kept, c), F32),
+            pltpu.VMEM((n, r - kept, c), F32),
+            pltpu.SemaphoreType.DMA((5,)),
+        ],
         compiler_params=params(),
         cost_estimate=cost(n * r * c, 8 * n * r * c),
         name="spread",
@@ -236,7 +239,7 @@
     groups = BLOCK // 8
     row = lax.broadcasted_iota(jnp.int32, (8, 128), 0)
     lane = lax.broadcasted_iota(jnp.int32, (8, 128), 1)
-    x = [jnp.where(lane == row + 8 * g, 1.0, 0.0) for g in range(groups)]
+    x = [jnp.where(lane % BLOCK == row + 8 * g, 1.0, 0.0) for g in range(groups)]
     c = [
         {g: jnp.broadcast_to(d[8 * g : 8 * g + 8, k : k + 1], (8, 128)) for g in range(k // 8, groups)}
         for k in range(BLOCK)
@@ -257,6 +260,35 @@
     return jnp.concatenate(x, axis=0)
 
 
+def pieces(x):
+    high = x.astype(BF16)
+    rest = x - high.astype(F32)
+    mid = rest.astype(BF16)
+    return high, mid, (rest - mid.astype(F32)).astype(BF16)
+
+
+def stack(x, order):
+    parts = pieces(x)
+    return jnp.concatenate([parts[i] for i in order], axis=0)
+
+
+LEFT = (0, 0, 1, 0, 2, 1)
+RIGHT = (0, 1, 0, 2, 0, 1)
+
+
+def beside(x):
+    parts = [p.astype(F32) for p in pieces(x)]
+    place = lax.broadcasted_iota(jnp.int32, x.shape, 1) // BLOCK
+    per = 128 // BLOCK
+    out = []
+    for start in range(0, len(LEFT), per):
+        wide = parts[LEFT[start]]
+        for i, which in enumerate(LEFT[start : start + per]):
+            wide = jnp.where(place == i, parts[which], wide)
+        out.append(wide[:, : BLOCK * len(LEFT[start : start + per])])
+    return jnp.concatenate(out, axis=1).astype(BF16)
+
+
 def lower_inverse(m_ref):
     k = m_ref.shape[0]
     lane = lax.broadcasted_iota(jnp.int32, (BLOCK, k), 1)
@@ -265,20 +297,19 @@
         lo = b * BLOCK
         hi = lo + BLOCK
         r = m_ref[lo:hi, :]
-        x = small_inverse(r[:, lo:hi])[:, :BLOCK]
+        x = small_inverse(r[:, lo:hi])
         inside = jnp.logical_and(lane >= lo, lane < hi)
         r = jnp.where(inside, jnp.where(lane - lo == row, 1.0, 0.0), r)
-        t = jnp.dot(x, r, precision=HIGH, preferred_element_type=F32)
+        t = jnp.dot(beside(x), stack(r, RIGHT), preferred_element_type=F32)
         m_ref[lo:hi, :] = jnp.where(lane < hi, t, 0.0)
+        if hi < k:
+            left, right = stack(t, LEFT), stack(t, RIGHT)
         for at, end in ((hi, min(hi + BLOCK, k)), (hi + BLOCK, k)):
             if at < end:
                 old = m_ref[at:end, :]
-                shape = old.shape
-                column = lax.broadcasted_iota(jnp.int32, shape, 1)
+                column = lax.broadcasted_iota(jnp.int32, old.shape, 1)
                 old = jnp.where(jnp.logical_and(column >= lo, column < hi), 0.0, old)
-                m_ref[at:end, :] = old - lax.dot_general(
-                    t[:, at:end], t, TN, precision=HIGH, preferred_element_type=F32
-                )
+                m_ref[at:end, :] = old - lax.dot_general(left[:, at:end], right, TN, preferred_element_type=F32)
 
 
 def finish_kernel(size, state_ref, sums_ref, half_ref, parts_ref, stale_ref, p_ref, basis_ref, new_ref, out_ref, m_ref):

time: 122 us -> 121 us (level)
  Pallas kernels: 28.5 us -> 27.2 us
where the time goes in v5:
time: 121 us; the launch traced here: 120 us
  blocking collectives  45.1 us (37%)
  waiting for transfers between devices  35 us (29%)
  Pallas kernels  27.2 us (22%)
  starting transfers between devices  11 us (9%)
  between operations  2.03 us (2%)
    all_to_all x2, blocking collectives, exchange(): return lax.all_to_all(blocks, axes, split_axis=0, concat_axis=0, tiled=True)  45.1 us
    all_to_all x2, waiting for transfers between devices, exchange(): return lax.all_to_all(blocks, axes, split_axis=0, concat_axis=0, tiled=True)  33.8 us
    pallas_call x1, Pallas kernels, first(): pl.pallas_call(first_kernel, in_specs=[SM, HBM, HBM], out_specs=VM, out_s...  11.6 us
    pallas_call x1, Pallas kernels, finish(): pl.pallas_call(functools.partial(finish_kernel, size), in_specs=[SM] + [V...  9.43 us
    all_to_all x2, starting transfers between devices, exchange(): return lax.all_to_all(blocks, axes, split_axis=0, concat_axis=0, tiled=True)  8.43 us
    pallas_call x1, Pallas kernels, power(): pl.pallas_call(power_kernel, in_specs=[VM, HBM, VM], out_specs=[VM, VM, V...  3.66 us
  transfers between devices with their start and end apart: 4, of which 3 were waited for; matrix products, arithmetic and copies ran while one was open for 0% of the time, Pallas kernels for 0%

profile of v5, /device:TPU:480, one launch (start us, length us, event | category | flops | bytes accessed | tf_op | source)
XLA Modules:
  0.0 120.5 jit_solution(6609325292503077275)
XLA Ops:
  1.9 0.1 add_convert_fusion.state_ref
  2.0 11.6 %first.1 = f32[16,264,128]{2,1,0:T(8,128)S(1)} custom-call(s32[3]{0:T(128)S(1)} %add_convert_fusion.state_ref, bf16[448,256]{1,0:T(8,128)(2,1)} %bitcast.7, bf16[448,2048]{1,0:T(8,128)(2,1)} %bitcast.5), custom_call_target="tpu_custom_call" | custom-call | flops 469762048 | bytes 4161536 | tf_op jit(solution)/shard_map/first/pallas_call | solution.py:86
  13.6 27.3 %all_to_all.20.in_ref = f32[16,264,128]{2,1,0:T(8,128)S(1)} all-to-all(f32[16,264,128]{2,1,0:T(8,128)S(1)} %first.1), channel_id=1, replica_groups=mesh['expert_0'=16,'expert_1'=2,'row_0'=4,'row_1'=4] {'row_0','row_1'}, dimensions={0} | all-to-all | bytes 4325376 | tf_op jit(solution)/shard_map/all_to_all | solution.py:357
  40.9 1.5 %spread.1 = (f32[256,128]{1,0:T(8,128)}, f32[8,128]{1,0:T(8,128)S(1)}, f32[16,256,128]{2,1,0:T(8,128)}) custom-call(f32[16,264,128]{2,1,0:T(8,128)S(1)} %all_to_all.20.in_ref), custom_call_target="tpu_custom_call" | custom-call | flops 540672 | bytes 4325376 | tf_op jit(solution)/shard_map/spread/pallas_call | solution.py:150
  42.4 0.0 copy-start
  42.4 4.6 %all-to-all-start.1 = ((f32[16,256,128]{2,1,0:T(8,128)}), f32[16,256,128]{2,1,0:T(8,128)}, u32[]{:S(2)}, u32[]{:S(2)}) async-start(f32[16,256,128]{2,1,0:T(8,128)} %get-tuple-element.17), calls=%async_computation.1 | async-start | bytes 4194304 | tf_op jit(solution)/shard_map/all_to_all | solution.py:357
  47.0 0.7 collective-permute-start
  47.7 0.0 collective-permute-done.extra_ref
  47.7 21.7 %all-to-all-done.1.w_hbm = f32[16,256,128]{2,1,0:T(8,128)} async-done(((f32[16,256,128]{2,1,0:T(8,128)}), f32[16,256,128]{2,1,0:T(8,128)}, u32[]{:S(2)}, u32[]{:S(2)}) %all-to-all-start.1) | async-done | bytes 2097184 | tf_op jit(solution)/shard_map/all_to_all | solution.py:357
  69.4 0.0 copy-done
  69.4 3.7 %power.1 = (bf16[448,256]{1,0:T(8,128)(2,1)S(1)}, f32[16,88,256]{2,1,0:T(8,128)S(1)}, f32[16,64,256]{2,1,0:T(8,128)S(1)}) custom-call(bf16[448,2048]{1,0:T(8,128)(2,1)S(1)} %bitcast.6, f32[16,256,128]{2,1,0:T(8,128)} %all-to-all-done.1.w_hbm, f32[8,128]{1,0:T(8,128)S(1)} %collective-permute-done.extra_ref), custom_call_target="tpu_custom_call" | custom-call | flops 939524096 | bytes 6029312 | tf_op jit(solution)/shard_map/power/pallas_call | solution.py:218
  73.1 17.8 %all_to_all.21.in_ref = f32[16,88,256]{2,1,0:T(8,128)S(1)} all-to-all(f32[16,88,256]{2,1,0:T(8,128)S(1)} %get-tuple-element.21), channel_id=1, replica_groups=mesh['expert_0'=16,'expert_1'=2,'row_0'=4,'row_1'=4] {'row_0','row_1'}, dimensions={0} | all-to-all | bytes 2883584 | tf_op jit(solution)/shard_map/all_to_all | solution.py:357
  90.9 1.1 share.1
  92.0 0.0 copy-start.1
  92.0 0.0 copy-start.2
  92.0 3.8 %all-to-all-start.3 = ((f32[16,80,256]{2,1,0:T(8,128)}), f32[16,80,256]{2,1,0:T(8,128)S(1)}, u32[]{:S(2)}, u32[]{:S(2)}) async-start(f32[16,80,256]{2,1,0:T(8,128)} %get-tuple-element.23), calls=%async_computation.3 | async-start | bytes 2621440 | tf_op jit(solution)/shard_map/all_to_all | solution.py:357
  95.9 1.9 %collective-permute-start.1 = (f32[8,128]{1,0:T(8,128)S(1)}, f32[8,128]{1,0:T(8,128)S(1)}, u32[]{:S(2)}, u32[]{:S(2)}) collective-permute-start(f32[8,128]{1,0:T(8,128)S(1)} %get-tuple-element.24), channel_id=1, source_target_pairs={{0,16},{16,0},{1,17},{17,1},{2,18},{18,2},{3,19},{19,3},{4,20},{20... | collective-permute-start | bytes 12296 | tf_op jit(solution)/shard_map/ppermute | solution.py:368
  97.8 1.1 collective-permute-done.1
  98.9 12.1 %all-to-all-done.3.parts_ref = f32[16,80,256]{2,1,0:T(8,128)S(1)} async-done(((f32[16,80,256]{2,1,0:T(8,128)}), f32[16,80,256]{2,1,0:T(8,128)S(1)}, u32[]{:S(2)}, u32[]{:S(2)}) %all-to-all-start.3) | async-done | bytes 1310752 | tf_op jit(solution)/shard_map/all_to_all | solution.py:357
  111.0 0.0 copy-done.1
  111.0 0.0 copy-done.2
  111.0 9.4 %finish.1 = (f32[448,256]{1,0:T(8,128)}, f32[256,128]{1,0:T(8,128)}) custom-call(s32[3]{0:T(128)S(1)} %add_convert_fusion.state_ref, f32[8,128]{1,0:T(8,128)S(1)} %add.3.sums_ref, f32[64,256]{1,0:T(8,128)S(1)} %get-tuple-element.26.half_ref, f32[16,80,256]{2,1,0:T(8,128)S(1)} %all-to-all-done.3.parts_ref, f32[256,128]{1,0:T(8,128)S(1)} %copy-done.2, ...), custom_call_target="tpu_custom_call" | custom-call | flops 6000000000 | bytes 458752 | tf_op jit(solution)/shard_map/finish/pallas_call | solution.py:344
  (1 shorter events, 0.0 us)
Async XLA Ops:
  42.4 27.0 %copy-start = (bf16[1,448,2048]{2,1,0:T(8,128)(2,1)S(1)}, bf16[1,448,2048]{2,1,0:T(8,128)(2,1)}, u32[]{:S(2)}) copy-start(bf16[1,448,2048]{2,1,0:T(8,128)(2,1)} %param.4) | copy-start | bytes 5505028
  42.4 27.0 %all-to-all-start.1 = ((f32[16,256,128]{2,1,0:T(8,128)}), f32[16,256,128]{2,1,0:T(8,128)}, u32[]{:S(2)}, u32[]{:S(2)}) async-start(f32[16,256,128]{2,1,0:T(8,128)} %get-tuple-element.17), calls=%async_computation.1 | async-start | bytes 4194304 | tf_op jit(solution)/shard_map/all_to_all | solution.py:357
  47.0 0.7 collective-permute-start
  92.0 19.1 %copy-start.1 = (bf16[1,448,256]{2,1,0:T(8,128)(2,1)S(1)}, bf16[1,448,256]{2,1,0:T(8,128)(2,1)}, u32[]{:S(2)}) copy-start(bf16[1,448,256]{2,1,0:T(8,128)(2,1)} %param.5) | copy-start | bytes 688132
  92.0 19.0 %copy-start.2 = (f32[256,128]{1,0:T(8,128)S(1)}, f32[256,128]{1,0:T(8,128)}, u32[]{:S(2)}) copy-start(f32[256,128]{1,0:T(8,128)} %get-tuple-element.28.stale_ref) | copy-start | bytes 393220
  92.0 19.0 %all-to-all-start.3 = ((f32[16,80,256]{2,1,0:T(8,128)}), f32[16,80,256]{2,1,0:T(8,128)S(1)}, u32[]{:S(2)}, u32[]{:S(2)}) async-start(f32[16,80,256]{2,1,0:T(8,128)} %get-tuple-element.23), calls=%async_computation.3 | async-start | bytes 2621440 | tf_op jit(solution)/shard_map/all_to_all | solution.py:357
  95.9 3.1 %collective-permute-start.1 = (f32[8,128]{1,0:T(8,128)S(1)}, f32[8,128]{1,0:T(8,128)S(1)}, u32[]{:S(2)}, u32[]{:S(2)}) collective-permute-start(f32[8,128]{1,0:T(8,128)S(1)} %get-tuple-element.24), channel_id=1, source_target_pairs={{0,16},{16,0},{1,17},{17,1},{2,18},{18,2},{3,19},{19,3},{4,20},{20... | collective-permute-start | bytes 12296 | tf_op jit(solution)/shard_map/ppermute | solution.py:368

commit v6 on v5

--- a/solution.py
+++ b/solution.py
@@ -42,7 +42,7 @@
         out_ref[2 * i + h, top : top + k, 128:] = block[k:, :]
 
 
-def first_kernel(state_ref, left_hbm, g_hbm, out_ref, left_ref, g_ref, sem):
+def first_kernel(loads_ref, left_hbm, g_hbm, out_ref, left_ref, g_ref, sem):
     n = out_ref.shape[0]
     k = left_ref.shape[1]
     pairs = n // 2
@@ -55,7 +55,7 @@
         loads.append(pltpu.make_async_copy(g_hbm.at[:, cols], g_ref.at[:, cols], sem.at[i]))
         loads[-1].start()
 
-    @pl.when(state_ref[2] > 0)
+    @pl.when(lax.axis_index(EXPERT[1]) == 0)
     def _():
         pl.delay(STAGGER)
 
@@ -70,7 +70,7 @@
             out_ref[2 * i + h, :k, :] = both[:, 128 * h : 128 * (h + 1)]
         part = g_ref[:, 256 * i : 256 * (i + 1)].astype(F32)
         squares = squares + (part * part).reshape(-1, 8, 256).sum(axis=0)
-    live = state_ref[1] > 0
+    live = loads_ref[0] >= 1
     squares = squares[:, :128] + squares[:, 128:]
     squares = jnp.where(live, squares[:4, :] + squares[4:, :], 0.0)
     slot = jnp.where(live, jnp.full((4, 128), 1.0 / (4 * 128 * n), F32), 0.0)
@@ -79,7 +79,7 @@
         out_ref[j, k:, :] = extra
 
 
-def first(state, left, g):
+def first(loads, left, g):
     d, k = left.shape
     s = g.shape[1]
     n = s // 128
@@ -92,7 +92,7 @@
         compiler_params=params(),
         cost_estimate=cost(2 * d * k * s, 2 * d * (s + k) + 4 * k * s),
         name="first",
-    )(state, pltpu.with_memory_space_constraint(left, pltpu.HBM), pltpu.with_memory_space_constraint(g, pltpu.HBM))
+    )(loads, pltpu.with_memory_space_constraint(left, pltpu.HBM), pltpu.with_memory_space_constraint(g, pltpu.HBM))
 
 
 def share_kernel(top, in_ref, rest_ref, sums_ref, half_ref, out_ref, wide_ref, sem):
@@ -312,7 +312,9 @@
                 m_ref[at:end, :] = old - lax.dot_general(left[:, at:end], right, TN, preferred_element_type=F32)
 
 
-def finish_kernel(size, state_ref, sums_ref, half_ref, parts_ref, stale_ref, p_ref, basis_ref, new_ref, out_ref, m_ref):
+def finish_kernel(size, loads_ref, flags_ref, sums_ref, half_ref, parts_ref, stale_ref, p_ref, basis_ref, new_ref, out_ref, m_ref):
+    live = loads_ref[0] >= 1
+    refresh = jnp.logical_and(live, flags_ref[0] == 1)
     n = parts_ref.shape[0]
     k = m_ref.shape[0]
     top = k // n
@@ -329,28 +331,28 @@
         piece = rest.astype(BF16)
         rest = rest - piece.astype(F32)
         fresh = fresh + lax.dot_general(p, piece, NT, preferred_element_type=F32)
-    old = jnp.where(state_ref[1] > 0, basis_ref[...].astype(F32), 0.0)
-    new_ref[...] = jnp.where(state_ref[0] > 0, fresh, old)
+    old = jnp.where(live, basis_ref[...].astype(F32), 0.0)
+    new_ref[...] = jnp.where(refresh, fresh, old)
     turned = jnp.dot(inv, cross, precision=HIGH, preferred_element_type=F32)
     squares = jnp.sum(sums_ref[:4, :], axis=(0, 1), keepdims=True)
     slots = jnp.sum(sums_ref[4:, :], axis=(0, 1), keepdims=True)
     scale = lax.rsqrt(squares / (slots * size) + 1e-06)
-    stale = jnp.where(state_ref[1] > 0, stale_ref[...], 0.0)
-    out_ref[...] = jnp.where(state_ref[0] > 0, turned, stale) * scale
-
-
-def finish(size, state, sums, half, parts, stale, p, basis):
+    stale = jnp.where(live, stale_ref[...], 0.0)
+    out_ref[...] = jnp.where(refresh, turned, stale) * scale
+
+
+def finish(size, loads, flags, sums, half, parts, stale, p, basis):
     d, k = p.shape
     return pl.pallas_call(
         functools.partial(finish_kernel, size),
-        in_specs=[SM] + [VM] * 6,
+        in_specs=[SM, SM] + [VM] * 6,
         out_specs=[VM, VM],
         out_shape=[jax.ShapeDtypeStruct((d, k), F32), jax.ShapeDtypeStruct((k, 128), F32)],
         scratch_shapes=[pltpu.VMEM((k, k), F32)],
         compiler_params=params(),
         cost_estimate=cost(6e9, 4 * d * k),
         name="finish",
-    )(state, sums, half, parts, stale, p, basis)
+    )(loads, flags, sums, half, parts, stale, p, basis)
 
 
 def exchange(blocks, axes):
@@ -372,12 +374,8 @@
     g, b = grads[0], basis[0]
     k = b.shape[1]
     s = g.shape[1]
-    live = loads[0] >= 1
-    refresh = jnp.logical_and(live, flags[0] == 1)
-    late = lax.axis_index(EXPERT[1]) == 0
-    state = jnp.stack([refresh, live, late]).astype(jnp.int32)
-
-    received = exchange(first(state, b, g), ROW)
+
+    received = exchange(first(loads, b, g), ROW)
     n = received.shape[0]
     stale, plane, copies = spread(received, 8)
     planes = between_planes(plane)
@@ -386,7 +384,7 @@
     top = k // n
     sums, half, sent = share(exchange(sent, ROW), rest, top)
     received, sums = lax.optimization_barrier((exchange(sent, ROW), both_cores(sums)))
-    new_basis, rotated = finish(float(d_whole * s), state, sums, half, received, stale, p, b)
+    new_basis, rotated = finish(float(d_whole * s), loads, flags, sums, half, received, stale, p, b)
     return new_basis[None], rotated[None]
 
 

time: 121 us -> 119 us (0.983)
  no operation moved by 1% of the time
where the time goes in v6:
time: 119 us
  blocking collectives  45.1 us (38%)
  waiting for transfers between devices  34.3 us (29%)
  Pallas kernels  26.2 us (22%)
  starting transfers between devices  11 us (9%)
  between operations  2.02 us (2%)
    all_to_all x2, blocking collectives, exchange(): return lax.all_to_all(blocks, axes, split_axis=0, concat_axis=0, tiled=True)  45.1 us
    all_to_all x2, waiting for transfers between devices, exchange(): return lax.all_to_all(blocks, axes, split_axis=0, concat_axis=0, tiled=True)  33.8 us
    pallas_call x1, Pallas kernels, first(): pl.pallas_call(first_kernel, in_specs=[SM, HBM, HBM], out_specs=VM, out_s...  11.1 us
    pallas_call x1, Pallas kernels, finish(): pl.pallas_call(functools.partial(finish_kernel, size), in_specs=[SM, SM]...  8.88 us
    all_to_all x2, starting transfers between devices, exchange(): return lax.all_to_all(blocks, axes, split_axis=0, concat_axis=0, tiled=True)  8.43 us
    pallas_call x1, Pallas kernels, power(): pl.pallas_call(power_kernel, in_specs=[VM, HBM, VM], out_specs=[VM, VM, V...  3.65 us
  transfers between devices with their start and end apart: 4, of which 3 were waited for; matrix products, arithmetic and copies ran while one was open for 0% of the time, Pallas kernels for 0%

profile of v6, /device:TPU:480, one launch (start us, length us, event | category | flops | bytes accessed | tf_op | source)
XLA Modules:
  0.0 118.6 jit_solution(1389083758446034568)
XLA Ops:
  1.3 11.1 %first.1 = f32[16,264,128]{2,1,0:T(8,128)S(1)} custom-call(s32[1]{0:T(128)S(6)} %copy.6.loads_ref, bf16[448,256]{1,0:T(8,128)(2,1)} %bitcast.6, bf16[448,2048]{1,0:T(8,128)(2,1)} %bitcast.4), custom_call_target="tpu_custom_call" | custom-call | flops 469762048 | bytes 4161536 | tf_op jit(solution)/shard_map/first/pallas_call | solution.py:86
  12.3 27.3 %all_to_all.20.in_ref = f32[16,264,128]{2,1,0:T(8,128)S(1)} all-to-all(f32[16,264,128]{2,1,0:T(8,128)S(1)} %first.1), channel_id=1, replica_groups=mesh['expert_0'=16,'expert_1'=2,'row_0'=4,'row_1'=4] {'row_0','row_1'}, dimensions={0} | all-to-all | bytes 4325376 | tf_op jit(solution)/shard_map/all_to_all | solution.py:359
  39.7 1.5 %spread.1 = (f32[256,128]{1,0:T(8,128)}, f32[8,128]{1,0:T(8,128)S(1)}, f32[16,256,128]{2,1,0:T(8,128)}) custom-call(f32[16,264,128]{2,1,0:T(8,128)S(1)} %all_to_all.20.in_ref), custom_call_target="tpu_custom_call" | custom-call | flops 540672 | bytes 4325376 | tf_op jit(solution)/shard_map/spread/pallas_call | solution.py:150
  41.2 0.0 copy-start
  41.2 4.6 %all-to-all-start.1 = ((f32[16,256,128]{2,1,0:T(8,128)}), f32[16,256,128]{2,1,0:T(8,128)}, u32[]{:S(2)}, u32[]{:S(2)}) async-start(f32[16,256,128]{2,1,0:T(8,128)} %get-tuple-element.17), calls=%async_computation.1 | async-start | bytes 4194304 | tf_op jit(solution)/shard_map/all_to_all | solution.py:359
  45.8 0.7 collective-permute-start
  46.4 0.0 collective-permute-done.extra_ref
  46.4 21.7 %all-to-all-done.1.w_hbm = f32[16,256,128]{2,1,0:T(8,128)} async-done(((f32[16,256,128]{2,1,0:T(8,128)}), f32[16,256,128]{2,1,0:T(8,128)}, u32[]{:S(2)}, u32[]{:S(2)}) %all-to-all-start.1) | async-done | bytes 2097184 | tf_op jit(solution)/shard_map/all_to_all | solution.py:359
  68.1 0.0 copy-done
  68.1 3.7 %power.1 = (bf16[448,256]{1,0:T(8,128)(2,1)S(1)}, f32[16,88,256]{2,1,0:T(8,128)S(1)}, f32[16,64,256]{2,1,0:T(8,128)S(1)}) custom-call(bf16[448,2048]{1,0:T(8,128)(2,1)S(1)} %bitcast.5, f32[16,256,128]{2,1,0:T(8,128)} %all-to-all-done.1.w_hbm, f32[8,128]{1,0:T(8,128)S(1)} %collective-permute-done.extra_ref), custom_call_target="tpu_custom_call" | custom-call | flops 939524096 | bytes 6029312 | tf_op jit(solution)/shard_map/power/pallas_call | solution.py:218
  71.8 17.8 %all_to_all.21.in_ref = f32[16,88,256]{2,1,0:T(8,128)S(1)} all-to-all(f32[16,88,256]{2,1,0:T(8,128)S(1)} %get-tuple-element.21), channel_id=1, replica_groups=mesh['expert_0'=16,'expert_1'=2,'row_0'=4,'row_1'=4] {'row_0','row_1'}, dimensions={0} | all-to-all | bytes 2883584 | tf_op jit(solution)/shard_map/all_to_all | solution.py:359
  89.6 1.1 share.1
  90.7 0.0 copy-start.1
  90.7 0.0 copy-start.2
  90.7 3.8 %all-to-all-start.3 = ((f32[16,80,256]{2,1,0:T(8,128)}), f32[16,80,256]{2,1,0:T(8,128)S(1)}, u32[]{:S(2)}, u32[]{:S(2)}) async-start(f32[16,80,256]{2,1,0:T(8,128)} %get-tuple-element.23), calls=%async_computation.3 | async-start | bytes 2621440 | tf_op jit(solution)/shard_map/all_to_all | solution.py:359
  94.6 1.9 %collective-permute-start.1 = (f32[8,128]{1,0:T(8,128)S(1)}, f32[8,128]{1,0:T(8,128)S(1)}, u32[]{:S(2)}, u32[]{:S(2)}) collective-permute-start(f32[8,128]{1,0:T(8,128)S(1)} %get-tuple-element.24), channel_id=1, source_target_pairs={{0,16},{16,0},{1,17},{17,1},{2,18},{18,2},{3,19},{19,3},{4,20},{20... | collective-permute-start | bytes 12296 | tf_op jit(solution)/shard_map/ppermute | solution.py:370
  97.1 0.5 collective-permute-done.1
  97.6 12.1 %all-to-all-done.3.parts_ref = f32[16,80,256]{2,1,0:T(8,128)S(1)} async-done(((f32[16,80,256]{2,1,0:T(8,128)}), f32[16,80,256]{2,1,0:T(8,128)S(1)}, u32[]{:S(2)}, u32[]{:S(2)}) %all-to-all-start.3) | async-done | bytes 1310752 | tf_op jit(solution)/shard_map/all_to_all | solution.py:359
  109.8 0.0 copy-done.1
  109.8 0.0 copy-done.2
  109.8 8.9 %finish.1 = (f32[448,256]{1,0:T(8,128)}, f32[256,128]{1,0:T(8,128)}) custom-call(s32[1]{0:T(128)S(6)} %copy.6.loads_ref, s32[1]{0:T(128)S(6)} %copy.7.flags_ref, f32[8,128]{1,0:T(8,128)S(1)} %add.3.sums_ref, f32[64,256]{1,0:T(8,128)S(1)} %get-tuple-element.26.half_ref, f32[16,80,256]{2,1,0:T(8,128)S(1)} %all-to-all-done.3.parts_ref, ...), custom_call_target="tpu_custom_call" | custom-call | flops 6000000000 | bytes 458752 | tf_op jit(solution)/shard_map/finish/pallas_call | solution.py:346
  (1 shorter events, 0.0 us)
Async XLA Ops:
  41.2 27.0 %copy-start = (bf16[1,448,2048]{2,1,0:T(8,128)(2,1)S(1)}, bf16[1,448,2048]{2,1,0:T(8,128)(2,1)}, u32[]{:S(2)}) copy-start(bf16[1,448,2048]{2,1,0:T(8,128)(2,1)} %param.4) | copy-start | bytes 5505028
  41.2 27.0 %all-to-all-start.1 = ((f32[16,256,128]{2,1,0:T(8,128)}), f32[16,256,128]{2,1,0:T(8,128)}, u32[]{:S(2)}, u32[]{:S(2)}) async-start(f32[16,256,128]{2,1,0:T(8,128)} %get-tuple-element.17), calls=%async_computation.1 | async-start | bytes 4194304 | tf_op jit(solution)/shard_map/all_to_all | solution.py:359
  45.8 0.7 collective-permute-start
  90.7 19.1 %copy-start.1 = (bf16[1,448,256]{2,1,0:T(8,128)(2,1)S(1)}, bf16[1,448,256]{2,1,0:T(8,128)(2,1)}, u32[]{:S(2)}) copy-start(bf16[1,448,256]{2,1,0:T(8,128)(2,1)} %param.5) | copy-start | bytes 688132
  90.7 19.0 %copy-start.2 = (f32[256,128]{1,0:T(8,128)S(1)}, f32[256,128]{1,0:T(8,128)}, u32[]{:S(2)}) copy-start(f32[256,128]{1,0:T(8,128)} %get-tuple-element.28.stale_ref) | copy-start | bytes 393220
  90.7 19.0 %all-to-all-start.3 = ((f32[16,80,256]{2,1,0:T(8,128)}), f32[16,80,256]{2,1,0:T(8,128)S(1)}, u32[]{:S(2)}, u32[]{:S(2)}) async-start(f32[16,80,256]{2,1,0:T(8,128)} %get-tuple-element.23), calls=%async_computation.3 | async-start | bytes 2621440 | tf_op jit(solution)/shard_map/all_to_all | solution.py:359
  94.6 3.1 %collective-permute-start.1 = (f32[8,128]{1,0:T(8,128)S(1)}, f32[8,128]{1,0:T(8,128)S(1)}, u32[]{:S(2)}, u32[]{:S(2)}) collective-permute-start(f32[8,128]{1,0:T(8,128)S(1)} %get-tuple-element.24), channel_id=1, source_target_pairs={{0,16},{16,0},{1,17},{17,1},{2,18},{18,2},{3,19},{19,3},{4,20},{20... | collective-permute-start | bytes 12296 | tf_op jit(solution)/shard_map/ppermute | solution.py:370

commit v7 on v6

--- a/solution.py
+++ b/solution.py
@@ -247,11 +247,12 @@
     for j in range(BLOCK):
         gj, sj = j // 8, j % 8
         r = lax.rsqrt(sub(c[j][gj], sj))
+        inverse = r * r
         low = {g: c[j][g] * r for g in range(gj, groups)}
         for k in range(j + 1, BLOCK):
-            at = sub(low[k // 8], k % 8)
+            at = sub(c[j][k // 8], k % 8) * inverse
             for g in range(k // 8, groups):
-                c[k][g] = c[k][g] - low[g] * at
+                c[k][g] = c[k][g] - c[j][g] * at
         xr = sub(x[gj], sj) * r
         below = jnp.where(row > sj, low[gj], 0.0)
         x[gj] = jnp.where(row == sj, xr, x[gj] - below * xr)

time: 119 us -> 120 us (level)
  no operation moved by 1% of the time
where the time goes in v7:
time: 120 us; the launch traced here: 119 us
  blocking collectives  45.1 us (38%)
  waiting for transfers between devices  34.3 us (29%)
  Pallas kernels  26.8 us (22%)
  starting transfers between devices  11 us (9%)
  between operations  2.02 us (2%)
    all_to_all x2, blocking collectives, exchange(): return lax.all_to_all(blocks, axes, split_axis=0, concat_axis=0, tiled=True)  45.1 us
    all_to_all x2, waiting for transfers between devices, exchange(): return lax.all_to_all(blocks, axes, split_axis=0, concat_axis=0, tiled=True)  33.8 us
    pallas_call x1, Pallas kernels, first(): pl.pallas_call(first_kernel, in_specs=[SM, HBM, HBM], out_specs=VM, out_s...  11.1 us
    pallas_call x1, Pallas kernels, finish(): pl.pallas_call(functools.partial(finish_kernel, size), in_specs=[SM, SM]...  9.48 us
    all_to_all x2, starting transfers between devices, exchange(): return lax.all_to_all(blocks, axes, split_axis=0, concat_axis=0, tiled=True)  8.43 us
    pallas_call x1, Pallas kernels, power(): pl.pallas_call(power_kernel, in_specs=[VM, HBM, VM], out_specs=[VM, VM, V...  3.65 us
  transfers between devices with their start and end apart: 4, of which 3 were waited for; matrix products, arithmetic and copies ran while one was open for 0% of the time, Pallas kernels for 0%

profile of v7, /device:TPU:480, one launch (start us, length us, event | category | flops | bytes accessed | tf_op | source)
XLA Modules:
  0.0 119.2 jit_solution(8773129465409015781)
XLA Ops:
  1.3 11.1 %first.1 = f32[16,264,128]{2,1,0:T(8,128)S(1)} custom-call(s32[1]{0:T(128)S(6)} %copy.6.loads_ref, bf16[448,256]{1,0:T(8,128)(2,1)} %bitcast.6, bf16[448,2048]{1,0:T(8,128)(2,1)} %bitcast.4), custom_call_target="tpu_custom_call" | custom-call | flops 469762048 | bytes 4161536 | tf_op jit(solution)/shard_map/first/pallas_call | solution.py:86
  12.3 27.3 %all_to_all.20.in_ref = f32[16,264,128]{2,1,0:T(8,128)S(1)} all-to-all(f32[16,264,128]{2,1,0:T(8,128)S(1)} %first.1), channel_id=1, replica_groups=mesh['expert_0'=16,'expert_1'=2,'row_0'=4,'row_1'=4] {'row_0','row_1'}, dimensions={0} | all-to-all | bytes 4325376 | tf_op jit(solution)/shard_map/all_to_all | solution.py:360
  39.7 1.5 %spread.1 = (f32[256,128]{1,0:T(8,128)}, f32[8,128]{1,0:T(8,128)S(1)}, f32[16,256,128]{2,1,0:T(8,128)}) custom-call(f32[16,264,128]{2,1,0:T(8,128)S(1)} %all_to_all.20.in_ref), custom_call_target="tpu_custom_call" | custom-call | flops 540672 | bytes 4325376 | tf_op jit(solution)/shard_map/spread/pallas_call | solution.py:150
  41.2 0.0 copy-start
  41.2 4.6 %all-to-all-start.1 = ((f32[16,256,128]{2,1,0:T(8,128)}), f32[16,256,128]{2,1,0:T(8,128)}, u32[]{:S(2)}, u32[]{:S(2)}) async-start(f32[16,256,128]{2,1,0:T(8,128)} %get-tuple-element.17), calls=%async_computation.1 | async-start | bytes 4194304 | tf_op jit(solution)/shard_map/all_to_all | solution.py:360
  45.8 0.7 collective-permute-start
  46.4 0.0 collective-permute-done.extra_ref
  46.4 21.7 %all-to-all-done.1.w_hbm = f32[16,256,128]{2,1,0:T(8,128)} async-done(((f32[16,256,128]{2,1,0:T(8,128)}), f32[16,256,128]{2,1,0:T(8,128)}, u32[]{:S(2)}, u32[]{:S(2)}) %all-to-all-start.1) | async-done | bytes 2097184 | tf_op jit(solution)/shard_map/all_to_all | solution.py:360
  68.1 0.0 copy-done
  68.1 3.7 %power.1 = (bf16[448,256]{1,0:T(8,128)(2,1)S(1)}, f32[16,88,256]{2,1,0:T(8,128)S(1)}, f32[16,64,256]{2,1,0:T(8,128)S(1)}) custom-call(bf16[448,2048]{1,0:T(8,128)(2,1)S(1)} %bitcast.5, f32[16,256,128]{2,1,0:T(8,128)} %all-to-all-done.1.w_hbm, f32[8,128]{1,0:T(8,128)S(1)} %collective-permute-done.extra_ref), custom_call_target="tpu_custom_call" | custom-call | flops 939524096 | bytes 6029312 | tf_op jit(solution)/shard_map/power/pallas_call | solution.py:218
  71.8 17.8 %all_to_all.21.in_ref = f32[16,88,256]{2,1,0:T(8,128)S(1)} all-to-all(f32[16,88,256]{2,1,0:T(8,128)S(1)} %get-tuple-element.21), channel_id=1, replica_groups=mesh['expert_0'=16,'expert_1'=2,'row_0'=4,'row_1'=4] {'row_0','row_1'}, dimensions={0} | all-to-all | bytes 2883584 | tf_op jit(solution)/shard_map/all_to_all | solution.py:360
  89.6 1.1 share.1
  90.7 0.0 copy-start.1
  90.7 0.0 copy-start.2
  90.7 3.8 %all-to-all-start.3 = ((f32[16,80,256]{2,1,0:T(8,128)}), f32[16,80,256]{2,1,0:T(8,128)S(1)}, u32[]{:S(2)}, u32[]{:S(2)}) async-start(f32[16,80,256]{2,1,0:T(8,128)} %get-tuple-element.23), calls=%async_computation.3 | async-start | bytes 2621440 | tf_op jit(solution)/shard_map/all_to_all | solution.py:360
  94.6 1.9 %collective-permute-start.1 = (f32[8,128]{1,0:T(8,128)S(1)}, f32[8,128]{1,0:T(8,128)S(1)}, u32[]{:S(2)}, u32[]{:S(2)}) collective-permute-start(f32[8,128]{1,0:T(8,128)S(1)} %get-tuple-element.24), channel_id=1, source_target_pairs={{0,16},{16,0},{1,17},{17,1},{2,18},{18,2},{3,19},{19,3},{4,20},{20... | collective-permute-start | bytes 12296 | tf_op jit(solution)/shard_map/ppermute | solution.py:371
  97.1 0.5 collective-permute-done.1
  97.6 12.1 %all-to-all-done.3.parts_ref = f32[16,80,256]{2,1,0:T(8,128)S(1)} async-done(((f32[16,80,256]{2,1,0:T(8,128)}), f32[16,80,256]{2,1,0:T(8,128)S(1)}, u32[]{:S(2)}, u32[]{:S(2)}) %all-to-all-start.3) | async-done | bytes 1310752 | tf_op jit(solution)/shard_map/all_to_all | solution.py:360
  109.8 0.0 copy-done.1
  109.8 0.0 copy-done.2
  109.8 9.5 %finish.1 = (f32[448,256]{1,0:T(8,128)}, f32[256,128]{1,0:T(8,128)}) custom-call(s32[1]{0:T(128)S(6)} %copy.6.loads_ref, s32[1]{0:T(128)S(6)} %copy.7.flags_ref, f32[8,128]{1,0:T(8,128)S(1)} %add.3.sums_ref, f32[64,256]{1,0:T(8,128)S(1)} %get-tuple-element.26.half_ref, f32[16,80,256]{2,1,0:T(8,128)S(1)} %all-to-all-done.3.parts_ref, ...), custom_call_target="tpu_custom_call" | custom-call | flops 6000000000 | bytes 458752 | tf_op jit(solution)/shard_map/finish/pallas_call | solution.py:347
  (1 shorter events, 0.0 us)
Async XLA Ops:
  41.2 27.0 %copy-start = (bf16[1,448,2048]{2,1,0:T(8,128)(2,1)S(1)}, bf16[1,448,2048]{2,1,0:T(8,128)(2,1)}, u32[]{:S(2)}) copy-start(bf16[1,448,2048]{2,1,0:T(8,128)(2,1)} %param.4) | copy-start | bytes 5505028
  41.2 27.0 %all-to-all-start.1 = ((f32[16,256,128]{2,1,0:T(8,128)}), f32[16,256,128]{2,1,0:T(8,128)}, u32[]{:S(2)}, u32[]{:S(2)}) async-start(f32[16,256,128]{2,1,0:T(8,128)} %get-tuple-element.17), calls=%async_computation.1 | async-start | bytes 4194304 | tf_op jit(solution)/shard_map/all_to_all | solution.py:360
  45.8 0.7 collective-permute-start
  90.7 19.1 %copy-start.1 = (bf16[1,448,256]{2,1,0:T(8,128)(2,1)S(1)}, bf16[1,448,256]{2,1,0:T(8,128)(2,1)}, u32[]{:S(2)}) copy-start(bf16[1,448,256]{2,1,0:T(8,128)(2,1)} %param.5) | copy-start | bytes 688132
  90.7 19.0 %copy-start.2 = (f32[256,128]{1,0:T(8,128)S(1)}, f32[256,128]{1,0:T(8,128)}, u32[]{:S(2)}) copy-start(f32[256,128]{1,0:T(8,128)} %get-tuple-element.28.stale_ref) | copy-start | bytes 393220
  90.7 19.0 %all-to-all-start.3 = ((f32[16,80,256]{2,1,0:T(8,128)}), f32[16,80,256]{2,1,0:T(8,128)S(1)}, u32[]{:S(2)}, u32[]{:S(2)}) async-start(f32[16,80,256]{2,1,0:T(8,128)} %get-tuple-element.23), calls=%async_computation.3 | async-start | bytes 2621440 | tf_op jit(solution)/shard_map/all_to_all | solution.py:360
  94.6 3.1 %collective-permute-start.1 = (f32[8,128]{1,0:T(8,128)S(1)}, f32[8,128]{1,0:T(8,128)S(1)}, u32[]{:S(2)}, u32[]{:S(2)}) collective-permute-start(f32[8,128]{1,0:T(8,128)S(1)} %get-tuple-element.24), channel_id=1, source_target_pairs={{0,16},{16,0},{1,17},{17,1},{2,18},{18,2},{3,19},{19,3},{4,20},{20... | collective-permute-start | bytes 12296 | tf_op jit(solution)/shard_map/ppermute | solution.py:371
